TPU v7x, 256 devices: a whole 4x4x8 slice. The times are simulated.
256 devices in a mesh: dp: 4 (over x_hi, core), centre: 64 (over z, y, x_lo).
Axes of the slice: x: 4 (x_hi: 2, x_lo: 2; x = x_hi * 2 + x_lo), y: 4, z: 8, core: 2. Of those that a mesh axis runs over, the one named last changes fastest.
Arguments:
- samples: bfloat16 [16384, 128], P('dp'), may hold values from -24 to 24
- centres: bfloat16 [16384, 128], P('centre'), may hold values from -6 to 6
- facility_prior_logprob: float32 [16384], P('centre'), may hold values from -2 to 0
Outputs:
- new_centres: float32 [16384, 128], P('centre')
- new_log_prior: float32 [16384], P('centre')
- log_partition: float32 [16384], P('dp')
All inputs are finite; a program needn't handle non-finite values.
Results may differ from a plain program's by a relative error of at most 0.00075.
Values sent between devices are 32-bit elements; how exact they have to be, the bound alone decides.
No kernel may reach another device: no remote copies, remote signals or barrier semaphores. Data moves between devices by JAX's collectives and lax.ppermute only.
A program may use at most 64 MiB of HBM per device.

v0:
```python
import jax
import jax.numpy as jnp
from jax import lax
from jax.sharding import Mesh
from jax.sharding import PartitionSpec as P

CENTRE = ("centre_0", "centre_1", "centre_2")


inverse_coolness_beta = 0.0625


def collected_together(x, axis):
    leaves = jax.tree.leaves(x)
    sequence = sorted(range(len(leaves)), key=lambda k: -leaves[k].size)
    width = (1, *leaves[sequence[0]].shape)[-1]
    lines = [
        jnp.pad(leaves[k].reshape(-1), (0, -leaves[k].size % width)).reshape(-1, width)
        for k in sequence
    ]
    both, at, found = (lax.all_gather(jnp.concatenate(lines), axis), 0, {})
    for k, line in zip(sequence, lines):
        share = both[:, at : at + len(line)].reshape(len(both), -1)
        found[k] = share[:, : leaves[k].size].reshape(-1, *leaves[k].shape)
        at += len(line)
    numbers = iter(range(len(leaves)))
    return jax.tree.map(lambda _: found[next(numbers)], x)


def merged_by_axis(x, axes, combine):
    for axis in axes:
        pieces = collected_together(x, axis)
        x = jax.tree.map(lambda part: part[0], pieces)
        for k in range(1, lax.axis_size(axis)):
            x = combine(x, jax.tree.map(lambda part: part[k], pieces))
    return x


def copy_for_each(x, axis):
    copies = jnp.broadcast_to(x, (lax.axis_size(axis), *x.shape))
    return lax.all_to_all(copies, axis, split_axis=0, concat_axis=0, tiled=True)


def over_copies(x, axis):
    everything = copy_for_each(x, axis)
    return jnp.sum(everything, axis=0)


def together(arrays, axis):
    ends = [0]
    for a in arrays:
        ends.append(ends[-1] + a.size)
    so_far = over_copies(jnp.concatenate([a.ravel() for a in arrays]), axis)
    return tuple((so_far[b:e].reshape(a.shape) for a, b, e in zip(arrays, ends, ends[1:])))


def block_scores(rows_block, centres, facility_norm_sq, facility_prior_logprob):
    padded_row_width = rows_block.astype(jnp.float32)
    point_norm_sq = jnp.sum(padded_row_width * padded_row_width, axis=1)
    point_facility_inner = lax.dot_general(
        rows_block, centres, (((1,), (1,)), ((), ())), preferred_element_type=jnp.float32
    )
    return (
        facility_prior_logprob[None, :]
        - (point_norm_sq[:, None] - 2.0 * point_facility_inner + facility_norm_sq[None, :])
        * inverse_coolness_beta
    )


def split_blocks(rows):
    count_rows = rows.shape[0]
    block_rows = min(512, count_rows)
    return rows.reshape(count_rows // block_rows, block_rows, rows.shape[1])


def shard_sufficient_statistics(rows, centres, facility_norm_sq, facility_prior_logprob):

    def block_stats(rows_block):
        unnormalised_membership_energy = block_scores(
            rows_block, centres, facility_norm_sq, facility_prior_logprob
        )
        row_max = jnp.max(unnormalised_membership_energy, axis=1)
        row_total = jnp.sum(jnp.exp(unnormalised_membership_energy - row_max[:, None]), axis=1)
        return (row_max, row_total, unnormalised_membership_energy)

    blocks = split_blocks(rows)
    row_max, row_total, scores = lax.map(block_stats, blocks)
    return (row_max.reshape(rows.shape[0]), row_total.reshape(rows.shape[0]), scores, blocks)


def combine_partial(earlier, later):
    joint_max = jnp.maximum(earlier[0], later[0])
    joint_total = earlier[1] * jnp.exp(earlier[0] - joint_max) + later[1] * jnp.exp(
        later[0] - joint_max
    )
    return (joint_max, joint_total)


def accumulate(blocks, scores, partition, running):
    part_blocks = partition.reshape(blocks.shape[0], blocks.shape[1])

    def block_step(state, pieces):
        mass, weighted = state
        rows_block, unnormalised_membership_energy, part_block = pieces
        resp = jnp.exp(unnormalised_membership_energy - part_block[:, None]).astype(jnp.bfloat16)
        mass = mass + jnp.sum(resp, axis=0, dtype=jnp.float32)
        weighted = weighted + lax.dot_general(
            resp, rows_block, (((0,), (0,)), ((), ())), preferred_element_type=jnp.float32
        )
        return ((mass, weighted), None)

    result, unused = lax.scan(block_step, running, (blocks, scores, part_blocks))
    return result


def finish(weighted, mass, centres_wide, denominator):
    new_centres = (weighted + centres_wide) / (mass + 1.0)[:, None]
    new_log_prior = jnp.log((mass + 1.0) / denominator)
    return (new_centres, new_log_prior)


def shards(samples, centres, facility_prior_logprob):
    centres_wide = centres.astype(jnp.float32)
    facility_norm_sq = jnp.sum(centres_wide * centres_wide, axis=1)
    count_rows = samples.shape[0]
    local_centres = centres.shape[0]
    running = (
        jnp.zeros((local_centres,), jnp.float32),
        jnp.zeros((local_centres, samples.shape[1]), jnp.float32),
    )
    row_max, row_total, scores, blocks = shard_sufficient_statistics(
        samples, centres, facility_norm_sq, facility_prior_logprob
    )
    row_max, row_total = merged_by_axis((row_max, row_total), CENTRE, combine_partial)
    log_partition = row_max + jnp.log(row_total)
    running = accumulate(blocks, scores, log_partition, running)
    mass, weighted = running
    denominator = float(count_rows * lax.axis_size("dp") + local_centres * lax.axis_size(CENTRE))
    weighted, mass = together((weighted, mass), "dp")
    new_centres, new_log_prior = finish(weighted, mass, centres_wide, denominator)
    return (new_centres, new_log_prior, log_partition)


def solution(mesh):
    torus = Mesh(
        mesh.devices.reshape(mesh.shape["dp"], 8, 4, 2), ("dp", "centre_0", "centre_1", "centre_2")
    )
    in_specs = (P("dp", None), P(CENTRE, None), P(CENTRE))
    out_specs = (P(CENTRE, None), P(CENTRE), P("dp"))
    return jax.shard_map(
        shards, mesh=torus, in_specs=in_specs, out_specs=out_specs, check_vma=False
    )
```

profile of v0, /device:TPU:1, one launch (start us, length us, event | category | flops | bytes accessed | tf_op | source)
XLA Modules:
  0.0 116.1 jit_solution(4193583156859042970)
XLA Ops:
  0.7 1.0 fusion.15
  1.6 27.0 %while.27 = (s32[]{:T(128)}, f32[8,512]{1,0:T(8,128)S(1)}, f32[8,512]{1,0:T(8,128)S(1)}, f32[8,512,256]{1,2,0:T(8,128)}, f32[256]{0:T(256)}, /*index=5*/bf16[8,5...) while((s32[]{:T(128)}, f32[8,512]{1,0:T(8,128)S(1)}, ...), condition=%wide.region_5.6_spmd, body=%wide.region_1.5_spmd.sunk | while | flops 34798080 | bytes 2446449 | solution.py:87
  1.6 1.1 multiply_reduce_fusion.2
  2.7 1.2 %fusion.70 = (f32[512]{0:T(512)S(1)}, f32[512,256]{0,1:T(8,128)S(1)}) fusion(f32[256]{0:T(256)S(1)} %get-tuple-element.291, bf16[256,128]{1,0:T(8,128)(2,1)} %get-tuple-element.290, bf16[8,512,128]{2,1,0:T(8,128)(2,1)} %get-tuple-element.289, s32[]{:T(128)} %get-tuple-element.274, f32[512]{0:T(512)S(1)} %multiply_reduce_fusion.2, ...), kind=kOutput, calls=%fused_computation.112.clone.1 | convolution fusion | flops 34340352 | bytes 727552 | tf_op jit(solution)/shard_map/while/body/eval_jaxpr/dot_general | solution.py:60
  4.1 0.8 bitcast_dynamic-update-slice_fusion.2
  5.0 1.1 multiply_reduce_fusion.2
  6.1 1.2 %fusion.70 = (f32[512]{0:T(512)S(1)}, f32[512,256]{0,1:T(8,128)S(1)}) fusion(f32[256]{0:T(256)S(1)} %get-tuple-element.291, bf16[256,128]{1,0:T(8,128)(2,1)} %get-tuple-element.290, bf16[8,512,128]{2,1,0:T(8,128)(2,1)} %get-tuple-element.289, s32[]{:T(128)} %get-tuple-element.274, f32[512]{0:T(512)S(1)} %multiply_reduce_fusion.2, ...), kind=kOutput, calls=%fused_computation.112.clone.1 | convolution fusion | flops 34340352 | bytes 727552 | tf_op jit(solution)/shard_map/while/body/eval_jaxpr/dot_general | solution.py:60
  7.5 0.9 bitcast_dynamic-update-slice_fusion.2
  8.4 1.1 multiply_reduce_fusion.2
  9.4 1.2 %fusion.70 = (f32[512]{0:T(512)S(1)}, f32[512,256]{0,1:T(8,128)S(1)}) fusion(f32[256]{0:T(256)S(1)} %get-tuple-element.291, bf16[256,128]{1,0:T(8,128)(2,1)} %get-tuple-element.290, bf16[8,512,128]{2,1,0:T(8,128)(2,1)} %get-tuple-element.289, s32[]{:T(128)} %get-tuple-element.274, f32[512]{0:T(512)S(1)} %multiply_reduce_fusion.2, ...), kind=kOutput, calls=%fused_computation.112.clone.1 | convolution fusion | flops 34340352 | bytes 727552 | tf_op jit(solution)/shard_map/while/body/eval_jaxpr/dot_general | solution.py:60
  10.8 0.9 bitcast_dynamic-update-slice_fusion.2
  11.8 1.1 multiply_reduce_fusion.2
  12.8 1.2 %fusion.70 = (f32[512]{0:T(512)S(1)}, f32[512,256]{0,1:T(8,128)S(1)}) fusion(f32[256]{0:T(256)S(1)} %get-tuple-element.291, bf16[256,128]{1,0:T(8,128)(2,1)} %get-tuple-element.290, bf16[8,512,128]{2,1,0:T(8,128)(2,1)} %get-tuple-element.289, s32[]{:T(128)} %get-tuple-element.274, f32[512]{0:T(512)S(1)} %multiply_reduce_fusion.2, ...), kind=kOutput, calls=%fused_computation.112.clone.1 | convolution fusion | flops 34340352 | bytes 727552 | tf_op jit(solution)/shard_map/while/body/eval_jaxpr/dot_general | solution.py:60
  14.2 0.9 bitcast_dynamic-update-slice_fusion.2
  15.1 1.1 multiply_reduce_fusion.2
  16.2 1.2 %fusion.70 = (f32[512]{0:T(512)S(1)}, f32[512,256]{0,1:T(8,128)S(1)}) fusion(f32[256]{0:T(256)S(1)} %get-tuple-element.291, bf16[256,128]{1,0:T(8,128)(2,1)} %get-tuple-element.290, bf16[8,512,128]{2,1,0:T(8,128)(2,1)} %get-tuple-element.289, s32[]{:T(128)} %get-tuple-element.274, f32[512]{0:T(512)S(1)} %multiply_reduce_fusion.2, ...), kind=kOutput, calls=%fused_computation.112.clone.1 | convolution fusion | flops 34340352 | bytes 727552 | tf_op jit(solution)/shard_map/while/body/eval_jaxpr/dot_general | solution.py:60
  17.6 0.8 bitcast_dynamic-update-slice_fusion.2
  18.5 1.1 multiply_reduce_fusion.2
  19.6 1.2 %fusion.70 = (f32[512]{0:T(512)S(1)}, f32[512,256]{0,1:T(8,128)S(1)}) fusion(f32[256]{0:T(256)S(1)} %get-tuple-element.291, bf16[256,128]{1,0:T(8,128)(2,1)} %get-tuple-element.290, bf16[8,512,128]{2,1,0:T(8,128)(2,1)} %get-tuple-element.289, s32[]{:T(128)} %get-tuple-element.274, f32[512]{0:T(512)S(1)} %multiply_reduce_fusion.2, ...), kind=kOutput, calls=%fused_computation.112.clone.1 | convolution fusion | flops 34340352 | bytes 727552 | tf_op jit(solution)/shard_map/while/body/eval_jaxpr/dot_general | solution.py:60
  21.0 0.9 bitcast_dynamic-update-slice_fusion.2
  21.9 1.1 multiply_reduce_fusion.2
  22.9 1.2 %fusion.70 = (f32[512]{0:T(512)S(1)}, f32[512,256]{0,1:T(8,128)S(1)}) fusion(f32[256]{0:T(256)S(1)} %get-tuple-element.291, bf16[256,128]{1,0:T(8,128)(2,1)} %get-tuple-element.290, bf16[8,512,128]{2,1,0:T(8,128)(2,1)} %get-tuple-element.289, s32[]{:T(128)} %get-tuple-element.274, f32[512]{0:T(512)S(1)} %multiply_reduce_fusion.2, ...), kind=kOutput, calls=%fused_computation.112.clone.1 | convolution fusion | flops 34340352 | bytes 727552 | tf_op jit(solution)/shard_map/while/body/eval_jaxpr/dot_general | solution.py:60
  25.2 1.1 multiply_reduce_fusion.2
  26.3 1.2 %fusion.70 = (f32[512]{0:T(512)S(1)}, f32[512,256]{0,1:T(8,128)S(1)}) fusion(f32[256]{0:T(256)S(1)} %get-tuple-element.291, bf16[256,128]{1,0:T(8,128)(2,1)} %get-tuple-element.290, bf16[8,512,128]{2,1,0:T(8,128)(2,1)} %get-tuple-element.289, s32[]{:T(128)} %get-tuple-element.274, f32[512]{0:T(512)S(1)} %multiply_reduce_fusion.2, ...), kind=kOutput, calls=%fused_computation.112.clone.1 | convolution fusion | flops 34340352 | bytes 727552 | tf_op jit(solution)/shard_map/while/body/eval_jaxpr/dot_general | solution.py:60
  27.7 0.9 bitcast_dynamic-update-slice_fusion.2
  28.7 23.3 %all-gather.3 = f32[8,2,4096]{2,1,0:T(2,128)S(1)} all-gather(f32[1,2,4096]{2,1,0:T(2,128)S(1)} %maximum_bitcast_fusion), channel_id=2, replica_groups=mesh['dp'=4,'centre_0'=8,'centre_1'=4,'centre_2'=2] {'centre_0'}, dimensions={0}, use_global_device_ids=true | all-gather | bytes 294912 | tf_op jit(solution)/shard_map/all_gather | solution.py:21
  52.4 9.8 %all-gather.4 = f32[4,2,4096]{2,1,0:T(2,128)S(1)} all-gather(f32[1,2,4096]{2,1,0:T(2,128)S(1)} %maximum_bitcast_fusion.1), channel_id=3, replica_groups=mesh['dp'=4,'centre_0'=8,'centre_1'=4,'centre_2'=2] {'centre_1'}, dimensions={0}, use_global_device_ids=true | all-gather | bytes 163840 | tf_op jit(solution)/shard_map/all_gather | solution.py:21
  62.4 3.4 %all-gather.5 = f32[2,2,4096]{2,1,0:T(2,128)S(1)} all-gather(f32[1,2,4096]{2,1,0:T(2,128)S(1)} %maximum_bitcast_fusion.2), channel_id=4, replica_groups=mesh['dp'=4,'centre_0'=8,'centre_1'=4,'centre_2'=2] {'centre_2'}, dimensions={0}, use_global_device_ids=true | all-gather | bytes 98304 | tf_op jit(solution)/shard_map/all_gather | solution.py:21
  66.1 22.7 %while.28 = (s32[]{:T(128)}, f32[256]{0:T(256)S(1)}, f32[256,128]{1,0:T(8,128)S(1)}, f32[8,512,256]{1,2,0:T(8,128)}, f32[8,512]{1,0:T(8,128)S(1)}, /*index=5*/bf16[8,512,128]{2,1,0:T(8,128)(2,1)}, s32[]{:T(128)}, s32[]{:T(128)}) while((s32[]{:T(128)}, f32[256]{0:T(256)S(1)}, f32[256,128]{1,0:T(8,128)S(1)}, ...), condition=%wide.region_8.9_spmd.clone, body=%wide.region_6.8_spmd.clone.sunk | while | flops 34406656 | bytes 3551848 | solution.py:112
  66.2 1.1 constant_dynamic-slice_fusion.4
  67.5 1.3 %convolution_add_fusion.2 = f32[256,128]{1,0:T(8,128)S(1)} fusion(f32[1,512,256]{2,1,0:T(8,128)S(1)} %copy.18, f32[512]{0:T(512)S(1)} %bitcast.298, f32[256,128]{1,0:T(8,128)S(1)} %get-tuple-element.304, bf16[8,512,128]{2,1,0:T(8,128)(2,1)} %get-tuple-element.315, s32[]{:T(128)} %get-tuple-element.302, pred[]{:T(512)S(6)} %compare.3), kind=kOutput, calls=%fused_computation.11.clone.1 | convolution fusion | flops 33882112 | bytes 920065 | tf_op jit(solution)/shard_map/while/body/eval_jaxpr/dot_general | solution.py:107
  69.0 1.1 constant_dynamic-slice_fusion.4
  70.3 1.3 %convolution_add_fusion.2 = f32[256,128]{1,0:T(8,128)S(1)} fusion(f32[1,512,256]{2,1,0:T(8,128)S(1)} %copy.18, f32[512]{0:T(512)S(1)} %bitcast.298, f32[256,128]{1,0:T(8,128)S(1)} %get-tuple-element.304, bf16[8,512,128]{2,1,0:T(8,128)(2,1)} %get-tuple-element.315, s32[]{:T(128)} %get-tuple-element.302, pred[]{:T(512)S(6)} %compare.3), kind=kOutput, calls=%fused_computation.11.clone.1 | convolution fusion | flops 33882112 | bytes 920065 | tf_op jit(solution)/shard_map/while/body/eval_jaxpr/dot_general | solution.py:107
  71.9 1.1 constant_dynamic-slice_fusion.4
  73.2 1.3 %convolution_add_fusion.2 = f32[256,128]{1,0:T(8,128)S(1)} fusion(f32[1,512,256]{2,1,0:T(8,128)S(1)} %copy.18, f32[512]{0:T(512)S(1)} %bitcast.298, f32[256,128]{1,0:T(8,128)S(1)} %get-tuple-element.304, bf16[8,512,128]{2,1,0:T(8,128)(2,1)} %get-tuple-element.315, s32[]{:T(128)} %get-tuple-element.302, pred[]{:T(512)S(6)} %compare.3), kind=kOutput, calls=%fused_computation.11.clone.1 | convolution fusion | flops 33882112 | bytes 920065 | tf_op jit(solution)/shard_map/while/body/eval_jaxpr/dot_general | solution.py:107
  74.7 1.1 constant_dynamic-slice_fusion.4
  76.0 1.3 %convolution_add_fusion.2 = f32[256,128]{1,0:T(8,128)S(1)} fusion(f32[1,512,256]{2,1,0:T(8,128)S(1)} %copy.18, f32[512]{0:T(512)S(1)} %bitcast.298, f32[256,128]{1,0:T(8,128)S(1)} %get-tuple-element.304, bf16[8,512,128]{2,1,0:T(8,128)(2,1)} %get-tuple-element.315, s32[]{:T(128)} %get-tuple-element.302, pred[]{:T(512)S(6)} %compare.3), kind=kOutput, calls=%fused_computation.11.clone.1 | convolution fusion | flops 33882112 | bytes 920065 | tf_op jit(solution)/shard_map/while/body/eval_jaxpr/dot_general | solution.py:107
  77.5 1.1 constant_dynamic-slice_fusion.4
  78.8 1.3 %convolution_add_fusion.2 = f32[256,128]{1,0:T(8,128)S(1)} fusion(f32[1,512,256]{2,1,0:T(8,128)S(1)} %copy.18, f32[512]{0:T(512)S(1)} %bitcast.298, f32[256,128]{1,0:T(8,128)S(1)} %get-tuple-element.304, bf16[8,512,128]{2,1,0:T(8,128)(2,1)} %get-tuple-element.315, s32[]{:T(128)} %get-tuple-element.302, pred[]{:T(512)S(6)} %compare.3), kind=kOutput, calls=%fused_computation.11.clone.1 | convolution fusion | flops 33882112 | bytes 920065 | tf_op jit(solution)/shard_map/while/body/eval_jaxpr/dot_general | solution.py:107
  80.4 1.1 constant_dynamic-slice_fusion.4
  81.7 1.3 %convolution_add_fusion.2 = f32[256,128]{1,0:T(8,128)S(1)} fusion(f32[1,512,256]{2,1,0:T(8,128)S(1)} %copy.18, f32[512]{0:T(512)S(1)} %bitcast.298, f32[256,128]{1,0:T(8,128)S(1)} %get-tuple-element.304, bf16[8,512,128]{2,1,0:T(8,128)(2,1)} %get-tuple-element.315, s32[]{:T(128)} %get-tuple-element.302, pred[]{:T(512)S(6)} %compare.3), kind=kOutput, calls=%fused_computation.11.clone.1 | convolution fusion | flops 33882112 | bytes 920065 | tf_op jit(solution)/shard_map/while/body/eval_jaxpr/dot_general | solution.py:107
  83.2 1.1 constant_dynamic-slice_fusion.4
  84.5 1.3 %convolution_add_fusion.2 = f32[256,128]{1,0:T(8,128)S(1)} fusion(f32[1,512,256]{2,1,0:T(8,128)S(1)} %copy.18, f32[512]{0:T(512)S(1)} %bitcast.298, f32[256,128]{1,0:T(8,128)S(1)} %get-tuple-element.304, bf16[8,512,128]{2,1,0:T(8,128)(2,1)} %get-tuple-element.315, s32[]{:T(128)} %get-tuple-element.302, pred[]{:T(512)S(6)} %compare.3), kind=kOutput, calls=%fused_computation.11.clone.1 | convolution fusion | flops 33882112 | bytes 920065 | tf_op jit(solution)/shard_map/while/body/eval_jaxpr/dot_general | solution.py:107
  86.0 1.1 constant_dynamic-slice_fusion.4
  87.3 1.3 %convolution_add_fusion.2 = f32[256,128]{1,0:T(8,128)S(1)} fusion(f32[1,512,256]{2,1,0:T(8,128)S(1)} %copy.18, f32[512]{0:T(512)S(1)} %bitcast.298, f32[256,128]{1,0:T(8,128)S(1)} %get-tuple-element.304, bf16[8,512,128]{2,1,0:T(8,128)(2,1)} %get-tuple-element.315, s32[]{:T(128)} %get-tuple-element.302, pred[]{:T(512)S(6)} %compare.3), kind=kOutput, calls=%fused_computation.11.clone.1 | convolution fusion | flops 33882112 | bytes 920065 | tf_op jit(solution)/shard_map/while/body/eval_jaxpr/dot_general | solution.py:107
  88.9 1.1 broadcast_in_dim.32
  89.9 14.9 %all-to-all-start = ((f32[4,1,33024]{2,1,0:T(1,128)}), f32[4,1,33024]{2,1,0:T(1,128)S(1)}, u32[]{:S(2)}, u32[]{:S(2)}) async-start(f32[4,1,33024]{2,1,0:T(1,128)} %broadcast_in_dim.32), calls=%async_computation | async-start | bytes 1056768 | tf_op jit(solution)/shard_map/all_to_all | solution.py:41
  105.5 8.8 %all-to-all-done = f32[4,1,33024]{2,1,0:T(1,128)S(1)} async-done(((f32[4,1,33024]{2,1,0:T(1,128)}), f32[4,1,33024]{2,1,0:T(1,128)S(1)}, u32[]{:S(2)}, u32[]{:S(2)}) %all-to-all-start) | async-done | bytes 528416 | tf_op jit(solution)/shard_map/all_to_all | solution.py:41
  (82 shorter events, 8.8 us)
Async XLA Ops:
  66.1 49.2 %copy-start = (bf16[256,128]{1,0:T(8,128)(2,1)S(1)}, bf16[256,128]{1,0:T(8,128)(2,1)}, u32[]{:S(2)}) copy-start(bf16[256,128]{1,0:T(8,128)(2,1)} %get-tuple-element.320) | copy-start | bytes 196612
  89.9 24.3 %all-to-all-start = ((f32[4,1,33024]{2,1,0:T(1,128)}), f32[4,1,33024]{2,1,0:T(1,128)S(1)}, u32[]{:S(2)}, u32[]{:S(2)}) async-start(f32[4,1,33024]{2,1,0:T(1,128)} %broadcast_in_dim.32), calls=%async_computation | async-start | bytes 1056768 | tf_op jit(solution)/shard_map/all_to_all | solution.py:41
where the time goes:
time: 117 us; the launch traced here: 116 us
  blocking collectives  36.5 us (31%)
  matrix products  20.5 us (18%)
  local copies, waits for them, and re-layouts  19.1 us (16%)
  starting transfers between devices  14.9 us (13%)
  other arithmetic  14.8 us (13%)
  waiting for transfers between devices  8.76 us (7%)
    all_gather x3, blocking collectives, collected_together(): both, at, found = (lax.all_gather(jnp.concatenate(lines), axis), 0, {})  36.5 us
    all_to_all x1, starting transfers between devices, copy_for_each(): return lax.all_to_all(copies, axis, split_axis=0, concat_axis=0, tiled=True)  14.9 us
    dot_general x8, matrix products, block_step(): lax.dot_general(resp, rows_block, (((0,), (0,)), ((), ())), preferred_ele...  10.6 us
    dynamic_slice x24, local copies, waits for them, and re-layouts, accumulate(): lax.scan(block_step, running, (blocks, scores, part_blocks))  10.3 us
    dot_general x8, matrix products, block_scores(): lax.dot_general(rows_block, centres, (((1,), (1,)), ((), ())), preferred_...  9.87 us
    all_to_all x1, waiting for transfers between devices, copy_for_each(): return lax.all_to_all(copies, axis, split_axis=0, concat_axis=0, tiled=True)  8.76 us
    reduce_sum x8, other arithmetic, block_scores(): point_norm_sq = jnp.sum(padded_row_width * padded_row_width, axis=1)  8.42 us
    dynamic_update_slice x24, local copies, waits for them, and re-layouts, shard_sufficient_statistics(): row_max, row_total, scores = lax.map(block_stats, blocks)  7.47 us
  transfers between devices with their start and end apart: 1, of which 1 were waited for; matrix products, arithmetic and copies ran while one was open for 1% of the time, Pallas kernels for 0%

commit v1 on v0

v1 whole, which is shorter than its diff:
```python
import jax
import jax.numpy as jnp
import numpy as np
from jax import lax
from jax.experimental import pallas as pl
from jax.experimental.pallas import tpu as pltpu
from jax.sharding import Mesh
from jax.sharding import PartitionSpec as P

AXES = ("xh", "core", "z", "y", "xl")
DP = ("xh", "core")
CENTRE = ("z", "y", "xl")

inverse_coolness_beta = 0.0625
LOG2E = float(np.log2(np.e))
LN2 = float(np.log(2.0))
CROSS2 = 2.0 * inverse_coolness_beta * LOG2E

LANES = 128
TILE = 256


def column_of(row):
    return jnp.transpose(jnp.broadcast_to(row, (LANES, LANES)))


def centre_bias(centres_ref, prior_ref):
    wide = centres_ref[...].astype(jnp.float32)
    norm = jnp.sum(wide * wide, axis=1, keepdims=True)
    prior = jnp.concatenate([column_of(prior_ref[k : k + 1, :]) for k in range(prior_ref.shape[0])])
    return (prior - norm * inverse_coolness_beta) * LOG2E


def cross_tile(centres_ref, rows):
    return lax.dot_general(
        centres_ref[...], rows, (((1,), (1,)), ((), ())), preferred_element_type=jnp.float32
    )


def stats_kernel(samples_ref, centres_ref, prior_ref, out_ref):
    bias = centre_bias(centres_ref, prior_ref)
    for t in range(samples_ref.shape[0] // TILE):
        cross = cross_tile(centres_ref, samples_ref[t * TILE : (t + 1) * TILE, :])
        for h in range(TILE // LANES):
            score = cross[:, h * LANES : (h + 1) * LANES] * CROSS2 + bias
            top = jnp.max(score, axis=0, keepdims=True)
            total = jnp.sum(jnp.exp2(score - top), axis=0, keepdims=True)
            at = t * (TILE // LANES) + h
            out_ref[at : at + 1, :] = top + jnp.log2(total)


def accumulate_kernel(samples_ref, centres_ref, prior_ref, partition_ref, out_ref):
    bias = centre_bias(centres_ref, prior_ref)
    local = centres_ref.shape[0]
    weighted = jnp.zeros((local, LANES), jnp.float32)
    mass = jnp.zeros((local, LANES), jnp.float32)
    for t in range(samples_ref.shape[0] // TILE):
        rows = samples_ref[t * TILE : (t + 1) * TILE, :]
        cross = cross_tile(centres_ref, rows)
        for h in range(TILE // LANES):
            at = t * (TILE // LANES) + h
            score = cross[:, h * LANES : (h + 1) * LANES] * CROSS2 + bias
            resp = jnp.exp2(score - partition_ref[at : at + 1, :]).astype(jnp.bfloat16)
            mass = mass + resp.astype(jnp.float32)
            weighted = weighted + lax.dot_general(
                resp,
                rows[h * LANES : (h + 1) * LANES, :],
                (((1,), (0,)), ((), ())),
                preferred_element_type=jnp.float32,
            )
    out_ref[0:local, :] = weighted
    out_ref[local:, :] = jnp.zeros((out_ref.shape[0] - local, LANES), jnp.float32)
    for k in range(local // LANES):
        block = jnp.transpose(mass[k * LANES : (k + 1) * LANES, :])
        out_ref[local + k : local + k + 1, :] = jnp.sum(block, axis=0, keepdims=True)


def finish_kernel(denominator, mine_ref, other_ref, centres_ref, new_ref, prior_ref):
    local = centres_ref.shape[0]
    for k in range(local // LANES):
        rows = slice(k * LANES, (k + 1) * LANES)
        at = slice(local + k, local + k + 1)
        mass = mine_ref[at, :] + other_ref[at, :] + 1.0
        prior_ref[k : k + 1, :] = jnp.log(mass / denominator)
        weighted = mine_ref[rows, :] + other_ref[rows, :]
        new_ref[rows, :] = (weighted + centres_ref[rows, :].astype(jnp.float32)) / column_of(mass)


def shared(x, axes):
    n = lax.axis_size(axes)
    return lax.all_to_all(jnp.broadcast_to(x, (n, *x.shape)), axes, 0, 0, tiled=True)


def merged(parts):
    top = jnp.max(parts, axis=0)
    return top + jnp.log2(jnp.sum(jnp.exp2(parts - top), axis=0))


def swapped(x, axis):
    return lax.ppermute(x, axis, [(0, 1), (1, 0)])


def shards(samples, centres, facility_prior_logprob):
    rows, features = samples.shape
    local = centres.shape[0]
    prior = facility_prior_logprob.reshape(local // LANES, LANES)
    partition = pl.pallas_call(
        stats_kernel, out_shape=jax.ShapeDtypeStruct((rows // LANES, LANES), jnp.float32)
    )(samples, centres, prior)
    partition = merged(shared(partition, ("y", "xl")))
    partition = merged(shared(partition, "z"))
    sums = pl.pallas_call(
        accumulate_kernel, out_shape=jax.ShapeDtypeStruct((local + 8, features), jnp.float32)
    )(samples, centres, prior, partition)
    sums = sums + swapped(sums, "core")
    other = swapped(sums, "xh")
    wide = samples.astype(jnp.float32)
    norms = jnp.sum(wide * wide, axis=1)
    log_partition = partition.reshape(rows) * LN2 - norms * inverse_coolness_beta
    denominator = float(rows * lax.axis_size(DP) + local * lax.axis_size(CENTRE))
    new_centres, new_log_prior = pl.pallas_call(
        lambda *refs: finish_kernel(denominator, *refs),
        out_shape=(
            jax.ShapeDtypeStruct((local, features), jnp.float32),
            jax.ShapeDtypeStruct((local // LANES, LANES), jnp.float32),
        ),
    )(sums, other, centres)
    return new_centres, new_log_prior.reshape(local), log_partition


def solution(mesh):
    torus = Mesh(mesh.devices.reshape(2, 2, 8, 4, 2), AXES)
    in_specs = (P(DP, None), P(CENTRE, None), P(CENTRE))
    out_specs = (P(CENTRE, None), P(CENTRE), P(DP))
    return jax.shard_map(
        shards, mesh=torus, in_specs=in_specs, out_specs=out_specs, check_vma=False
    )
```

time: 117 us -> 51.7 us (0.44)
  blocking collectives: 36.5 us -> 11.3 us
  matrix products: 20.5 us -> 0 us
  local copies, waits for them, and re-layouts: 19.1 us -> 2.05 us
  other arithmetic: 14.8 us -> 2.27 us
  Pallas kernels: 0 us -> 8.48 us
  waiting for transfers between devices: 8.76 us -> 12.4 us
    all_gather x3 -> x0, blocking collectives: 36.5 us -> none  [collected_together(): both, at, found = (lax.all_gather(jnp.concatenate(lines), axis), 0, {})]
    dot_general x16 -> x0, matrix products: 20.5 us -> none  [the longest x8 10.6 us: block_step(): lax.dot_general(resp, rows_block, (((0,), (0,)), ((), ())), preferred_ele...]
    reduce_sum x26 -> x3, other arithmetic: 12 us -> 0.68 us  [the longest x1 0.61 us: shards(): norms = jnp.sum(wide * wide, axis=1)]
    all_to_all x0 -> x1, blocking collectives: none -> 11.3 us  [shared(): lax.all_to_all(jnp.broadcast_to(x, (n, *x.shape)), axes, 0, 0, tiled=True)]
    dynamic_slice x24 -> x0, local copies, waits for them, and re-layouts: 10.3 us -> none  [accumulate(): lax.scan(block_step, running, (blocks, scores, part_blocks))]
    pallas_call x0 -> x3, Pallas kernels: none -> 8.48 us  [the longest x1 3.43 us: shards(): pl.pallas_call(stats_kernel, out_shape=jax.ShapeDtypeStruct((rows // LANE...]
    dynamic_update_slice x24 -> x0, local copies, waits for them, and re-layouts: 7.47 us -> none  [shard_sufficient_statistics(): row_max, row_total, scores = lax.map(block_stats, blocks)]
    all_to_all x1, starting transfers between devices: 14.9 us -> 8.17 us  [shared(): lax.all_to_all(jnp.broadcast_to(x, (n, *x.shape)), axes, 0, 0, tiled=True)]
  transfers between devices with their start and end apart: 1 -> 3, of which waited for: 1 -> 3; matrix products, arithmetic and copies ran while one was open for 1% -> 1% of each run, Pallas kernels for 0% -> 0%
where the time goes in v1:
time: 51.7 us; the launch traced here: 51.4 us
  starting transfers between devices  14.1 us (27%)
  waiting for transfers between devices  12.4 us (24%)
  blocking collectives  11.3 us (22%)
  Pallas kernels  8.48 us (16%)
  other arithmetic  2.27 us (4%)
  local copies, waits for them, and re-layouts  2.05 us (4%)
  between operations  0.69 us (1%)
    all_to_all x1, blocking collectives, shared(): lax.all_to_all(jnp.broadcast_to(x, (n, *x.shape)), axes, 0, 0, tiled=True)  11.3 us
    all_to_all x1, starting transfers between devices, shared(): lax.all_to_all(jnp.broadcast_to(x, (n, *x.shape)), axes, 0, 0, tiled=True)  8.17 us
    all_to_all x1, waiting for transfers between devices, shared(): lax.all_to_all(jnp.broadcast_to(x, (n, *x.shape)), axes, 0, 0, tiled=True)  7.4 us
    ppermute x2, starting transfers between devices, swapped(): return lax.ppermute(x, axis, [(0, 1), (1, 0)])  5.95 us
    ppermute x2, waiting for transfers between devices, swapped(): return lax.ppermute(x, axis, [(0, 1), (1, 0)])  5.04 us
    pallas_call x1, Pallas kernels, shards(): pl.pallas_call(stats_kernel, out_shape=jax.ShapeDtypeStruct((rows // LANE...  3.43 us
    pallas_call x1, Pallas kernels, shards(): pl.pallas_call(accumulate_kernel, out_shape=jax.ShapeDtypeStruct((local +...  3.31 us
    pallas_call x1, Pallas kernels, shards(): pl.pallas_call(lambda *refs: finish_kernel(denominator, *refs), out_shape...  1.74 us
  transfers between devices with their start and end apart: 3, of which 3 were waited for; matrix products, arithmetic and copies ran while one was open for 1% of the time, Pallas kernels for 0%

profile of v1, /device:TPU:1, one launch (start us, length us, event | category | flops | bytes accessed | tf_op | source)
XLA Modules:
  0.0 51.4 jit_solution(14579384778382743372)
XLA Ops:
  0.6 0.0 copy-start
  0.6 3.4 %shard_map.58 = f32[32,128]{1,0:T(8,128)} custom-call(bf16[4096,128]{1,0:T(8,128)(2,1)} %samples_ref.3, bf16[256,128]{1,0:T(8,128)(2,1)} %refs_2_.1, f32[2,128]{1,0:T(2,128)} %bitcast.4), custom_call_target="tpu_custom_call" | custom-call | tf_op jit(solution)/shard_map/pallas_call | solution.py:107
  4.1 0.7 %broadcast_in_dim.8 = f32[8,32,128]{2,1,0:T(8,128)S(1)} broadcast(f32[32,128]{1,0:T(8,128)} %shard_map.58), dimensions={1,2} | broadcast | bytes 147456 | tf_op jit(solution)/shard_map/broadcast_in_dim | solution.py:91
  4.8 11.3 %all_to_all.10 = f32[8,32,128]{2,1,0:T(8,128)S(1)} all-to-all(f32[8,32,128]{2,1,0:T(8,128)S(1)} %broadcast_in_dim.8), channel_id=1, replica_groups=mesh['xh'=2,'core'=2,'z'=8,'y'=4,'xl'=2] {'y','xl'}, dimensions={0} | all-to-all | bytes 262144 | tf_op jit(solution)/shard_map/all_to_all | solution.py:91
  16.2 0.7 %broadcast_in_dim.9 = f32[8,32,128]{2,1,0:T(8,128)} broadcast(f32[32,128]{1,0:T(8,128)S(1)} %multiply_add_fusion.1), dimensions={1,2} | broadcast | bytes 147456 | tf_op jit(solution)/shard_map/broadcast_in_dim | solution.py:91
  16.8 8.2 %all-to-all-start.1 = ((f32[8,32,128]{2,1,0:T(8,128)}), f32[8,32,128]{2,1,0:T(8,128)S(1)}, u32[]{:S(2)}, u32[]{:S(2)}) async-start(f32[8,32,128]{2,1,0:T(8,128)} %broadcast_in_dim.9), calls=%async_computation.1 | async-start | bytes 262144 | tf_op jit(solution)/shard_map/all_to_all | solution.py:91
  25.0 0.0 copy-done
  25.0 0.6 %multiply_reduce_fusion = f32[4096]{0:T(1024)S(1)} fusion(bf16[4096,128]{1,0:T(8,128)(2,1)S(1)} %copy-done), kind=kLoop, calls=%fused_computation | loop fusion | flops 1568768 | bytes 1064960 | tf_op jit(solution)/shard_map/reduce_sum | solution.py:118
  25.6 7.4 %all-to-all-done.1 = f32[8,32,128]{2,1,0:T(8,128)S(1)} async-done(((f32[8,32,128]{2,1,0:T(8,128)}), f32[8,32,128]{2,1,0:T(8,128)S(1)}, u32[]{:S(2)}, u32[]{:S(2)}) %all-to-all-start.1) | async-done | bytes 131104 | tf_op jit(solution)/shard_map/all_to_all | solution.py:91
  33.1 0.6 %bitcast_subtract_fusion = (f32[4096]{0:T(1024)}, f32[32,128]{1,0:T(8,128)}) fusion(f32[4096]{0:T(1024)S(1)} %multiply_reduce_fusion, f32[32,128]{1,0:T(8,128)S(1)} %reduce_max.19, f32[32,128]{1,0:T(8,128)S(1)} %exponential_reduce_fusion), kind=kLoop, calls=%fused_computation.3 | loop fusion | flops 20480 | bytes 81920 | tf_op jit(solution)/shard_map/sub | solution.py:119
  33.7 3.3 %shard_map.59 = f32[264,128]{1,0:T(8,128)} custom-call(bf16[4096,128]{1,0:T(8,128)(2,1)} %samples_ref.3, bf16[256,128]{1,0:T(8,128)(2,1)} %refs_2_.1, f32[2,128]{1,0:T(2,128)} %bitcast.5, f32[32,128]{1,0:T(8,128)} %get-tuple-element.8.partition_ref), custom_call_target="tpu_custom_call" | custom-call | tf_op jit(solution)/shard_map/pallas_call | solution.py:112
  37.0 3.4 %collective-permute-start = (f32[264,128]{1,0:T(8,128)}, f32[264,128]{1,0:T(8,128)S(1)}, u32[]{:S(2)}, u32[]{:S(2)}) collective-permute-start(f32[264,128]{1,0:T(8,128)} %shard_map.59), channel_id=1, source_target_pairs={{0,64},{64,0},{1,65},{65,1},{2,66},{66,2},{3,67},{67,3},{4,68},{68... | collective-permute-start | bytes 405512 | tf_op jit(solution)/shard_map/ppermute | solution.py:100
  40.5 1.2 %collective-permute-done = f32[264,128]{1,0:T(8,128)S(1)} collective-permute-done((f32[264,128]{1,0:T(8,128)}, f32[264,128]{1,0:T(8,128)S(1)}, u32[]{:S(2)}, u32[]{:S(2)}) %collective-permute-start) | collective-permute-done | bytes 135200 | tf_op jit(solution)/shard_map/ppermute | solution.py:100
  41.7 0.9 %add.11.refs_0_ = f32[264,128]{1,0:T(8,128)S(1)} add(f32[264,128]{1,0:T(8,128)} %shard_map.59, f32[264,128]{1,0:T(8,128)S(1)} %collective-permute-done) | non-fusion elementwise | flops 33792 | bytes 405504 | tf_op jit(solution)/shard_map/add | solution.py:115
  42.6 0.0 copy-start.1
  42.6 2.5 %collective-permute-start.1 = (f32[264,128]{1,0:T(8,128)S(1)}, f32[264,128]{1,0:T(8,128)S(1)}, u32[]{:S(2)}, u32[]{:S(2)}) collective-permute-start(f32[264,128]{1,0:T(8,128)S(1)} %add.11.refs_0_), channel_id=1, source_target_pairs={{0,128},{128,0},{1,129},{129,1},{2,130},{130,2},{3,131},{131,3},{4... | collective-permute-start | bytes 405512 | tf_op jit(solution)/shard_map/ppermute | solution.py:100
  45.1 3.8 %collective-permute-done.1.refs_1_ = f32[264,128]{1,0:T(8,128)S(1)} collective-permute-done((f32[264,128]{1,0:T(8,128)S(1)}, f32[264,128]{1,0:T(8,128)S(1)}, u32[]{:S(2)}, u32[]{:S(2)}) %collective-permute-start.1) | collective-permute-done | bytes 135200 | tf_op jit(solution)/shard_map/ppermute | solution.py:100
  49.0 0.0 copy-done.1
  49.0 0.0 copy-start.2
  49.0 0.6 %copy-done.2 = f32[264,128]{1,0:T(8,128)} copy-done((f32[264,128]{1,0:T(8,128)}, f32[264,128]{1,0:T(8,128)S(1)}, u32[]{:S(2)}) %copy-start.2) | copy-done | bytes 135192
  49.6 1.7 %shard_map.60 = (f32[256,128]{1,0:T(8,128)}, f32[2,128]{1,0:T(2,128)}) custom-call(f32[264,128]{1,0:T(8,128)} %copy-done.1, f32[264,128]{1,0:T(8,128)} %copy-done.2, bf16[256,128]{1,0:T(8,128)(2,1)} %refs_2_.1), custom_call_target="tpu_custom_call" | custom-call | tf_op jit(solution)/shard_map/pallas_call | solution.py:121
  (5 shorter events, 0.1 us)
Async XLA Ops:
  0.6 24.4 %copy-start = (bf16[4096,128]{1,0:T(8,128)(2,1)S(1)}, bf16[4096,128]{1,0:T(8,128)(2,1)}, u32[]{:S(2)}) copy-start(bf16[4096,128]{1,0:T(8,128)(2,1)} %samples_ref.3) | copy-start | bytes 3145732
  16.8 16.2 %all-to-all-start.1 = ((f32[8,32,128]{2,1,0:T(8,128)}), f32[8,32,128]{2,1,0:T(8,128)S(1)}, u32[]{:S(2)}, u32[]{:S(2)}) async-start(f32[8,32,128]{2,1,0:T(8,128)} %broadcast_in_dim.9), calls=%async_computation.1 | async-start | bytes 262144 | tf_op jit(solution)/shard_map/all_to_all | solution.py:91
  37.0 4.6 %collective-permute-start = (f32[264,128]{1,0:T(8,128)}, f32[264,128]{1,0:T(8,128)S(1)}, u32[]{:S(2)}, u32[]{:S(2)}) collective-permute-start(f32[264,128]{1,0:T(8,128)} %shard_map.59), channel_id=1, source_target_pairs={{0,64},{64,0},{1,65},{65,1},{2,66},{66,2},{3,67},{67,3},{4,68},{68... | collective-permute-start | bytes 405512 | tf_op jit(solution)/shard_map/ppermute | solution.py:100
  42.6 6.4 %copy-start.1 = (f32[264,128]{1,0:T(8,128)}, f32[264,128]{1,0:T(8,128)S(1)}, u32[]{:S(2)}) copy-start(f32[264,128]{1,0:T(8,128)S(1)} %add.11.refs_0_) | copy-start | bytes 405508
  42.6 6.4 %collective-permute-start.1 = (f32[264,128]{1,0:T(8,128)S(1)}, f32[264,128]{1,0:T(8,128)S(1)}, u32[]{:S(2)}, u32[]{:S(2)}) collective-permute-start(f32[264,128]{1,0:T(8,128)S(1)} %add.11.refs_0_), channel_id=1, source_target_pairs={{0,128},{128,0},{1,129},{129,1},{2,130},{130,2},{3,131},{131,3},{4... | collective-permute-start | bytes 405512 | tf_op jit(solution)/shard_map/ppermute | solution.py:100
  49.0 0.7 %copy-start.2 = (f32[264,128]{1,0:T(8,128)}, f32[264,128]{1,0:T(8,128)S(1)}, u32[]{:S(2)}) copy-start(f32[264,128]{1,0:T(8,128)S(1)} %collective-permute-done.1.refs_1_) | copy-start | bytes 405508

commit v2 on v1

--- a/solution.py
+++ b/solution.py
@@ -6,6 +6,7 @@
 from jax.experimental.pallas import tpu as pltpu
 from jax.sharding import Mesh
 from jax.sharding import PartitionSpec as P
+
 
 AXES = ("xh", "core", "z", "y", "xl")
 DP = ("xh", "core")
@@ -18,6 +19,7 @@
 
 LANES = 128
 TILE = 256
+CHUNKS = 4
 
 
 def column_of(row):
@@ -37,20 +39,37 @@
     )
 
 
-def stats_kernel(samples_ref, centres_ref, prior_ref, out_ref):
+def stats_kernel(
+    samples_hbm, centres_ref, prior_ref, out_ref, samples_ref, kept_ref, bias_ref, sems
+):
+    step = samples_ref.shape[0] // CHUNKS
+    copies = []
+    for k in range(CHUNKS):
+        rows = pl.ds(k * step, step)
+        copies.append(
+            pltpu.make_async_copy(samples_hbm.at[rows, :], samples_ref.at[rows, :], sems.at[k])
+        )
+        copies[k].start()
     bias = centre_bias(centres_ref, prior_ref)
+    bias_ref[...] = bias
+    kept_ref[...] = centres_ref[...]
     for t in range(samples_ref.shape[0] // TILE):
+        if t * TILE % step == 0:
+            copies[t * TILE // step].wait()
         cross = cross_tile(centres_ref, samples_ref[t * TILE : (t + 1) * TILE, :])
         for h in range(TILE // LANES):
             score = cross[:, h * LANES : (h + 1) * LANES] * CROSS2 + bias
             top = jnp.max(score, axis=0, keepdims=True)
             total = jnp.sum(jnp.exp2(score - top), axis=0, keepdims=True)
             at = t * (TILE // LANES) + h
-            out_ref[at : at + 1, :] = top + jnp.log2(total)
+            out_ref[0, at : at + 1, :] = top + jnp.log2(total)
+    for k in range(1, out_ref.shape[0]):
+        out_ref[k, :, :] = out_ref[0, :, :]
 
 
-def accumulate_kernel(samples_ref, centres_ref, prior_ref, partition_ref, out_ref):
-    bias = centre_bias(centres_ref, prior_ref)
+def accumulate_kernel(samples_ref, centres_ref, bias_ref, parts_ref, out_ref, partition_ref):
+    bias = bias_ref[...]
+    partition_ref[...] = merged(parts_ref[...])
     local = centres_ref.shape[0]
     weighted = jnp.zeros((local, LANES), jnp.float32)
     mass = jnp.zeros((local, LANES), jnp.float32)
@@ -86,9 +105,12 @@
         new_ref[rows, :] = (weighted + centres_ref[rows, :].astype(jnp.float32)) / column_of(mass)
 
 
-def shared(x, axes):
-    n = lax.axis_size(axes)
-    return lax.all_to_all(jnp.broadcast_to(x, (n, *x.shape)), axes, 0, 0, tiled=True)
+def shared(copies, axes):
+    return lax.all_to_all(copies, axes, 0, 0, tiled=True)
+
+
+def on_chip(x):
+    return pltpu.with_memory_space_constraint(x, pltpu.VMEM)
 
 
 def merged(parts):
@@ -104,27 +126,46 @@
     rows, features = samples.shape
     local = centres.shape[0]
     prior = facility_prior_logprob.reshape(local // LANES, LANES)
-    partition = pl.pallas_call(
-        stats_kernel, out_shape=jax.ShapeDtypeStruct((rows // LANES, LANES), jnp.float32)
+    lines = rows // LANES
+    near, far = ("y", "xl"), "z"
+    whole = pl.BlockSpec(memory_space=pltpu.VMEM)
+    copies, samples_here, centres_here, bias = pl.pallas_call(
+        stats_kernel,
+        in_specs=[pl.BlockSpec(memory_space=pl.ANY), whole, whole],
+        out_specs=[whole] * 4,
+        out_shape=(
+            pltpu.VMEM((lax.axis_size(near), lines, LANES), jnp.float32),
+            pltpu.VMEM((rows, features), samples.dtype),
+            pltpu.VMEM((local, features), centres.dtype),
+            pltpu.VMEM((local, LANES), jnp.float32),
+        ),
+        scratch_shapes=[pltpu.SemaphoreType.DMA((CHUNKS,))],
     )(samples, centres, prior)
-    partition = merged(shared(partition, ("y", "xl")))
-    partition = merged(shared(partition, "z"))
-    sums = pl.pallas_call(
-        accumulate_kernel, out_shape=jax.ShapeDtypeStruct((local + 8, features), jnp.float32)
-    )(samples, centres, prior, partition)
+    part = merged(shared(copies, near))
+    parts = shared(jnp.broadcast_to(part, (lax.axis_size(far), *part.shape)), far)
+    sums, partition = pl.pallas_call(
+        accumulate_kernel,
+        in_specs=[whole, whole, whole, whole],
+        out_specs=[whole, whole],
+        out_shape=(
+            pltpu.VMEM((local + 8, features), jnp.float32),
+            pltpu.VMEM((lines, LANES), jnp.float32),
+        ),
+    )(on_chip(samples_here), on_chip(centres_here), on_chip(bias), on_chip(parts))
     sums = sums + swapped(sums, "core")
     other = swapped(sums, "xh")
-    wide = samples.astype(jnp.float32)
+    wide = samples_here.astype(jnp.float32)
     norms = jnp.sum(wide * wide, axis=1)
     log_partition = partition.reshape(rows) * LN2 - norms * inverse_coolness_beta
     denominator = float(rows * lax.axis_size(DP) + local * lax.axis_size(CENTRE))
     new_centres, new_log_prior = pl.pallas_call(
         lambda *refs: finish_kernel(denominator, *refs),
+        in_specs=[whole, whole, whole],
         out_shape=(
             jax.ShapeDtypeStruct((local, features), jnp.float32),
             jax.ShapeDtypeStruct((local // LANES, LANES), jnp.float32),
         ),
-    )(sums, other, centres)
+    )(on_chip(sums), on_chip(other), on_chip(centres_here))
     return new_centres, new_log_prior.reshape(local), log_partition
 
 

time: 51.7 us -> 45.2 us (0.87)
  blocking collectives: 11.3 us -> 27.3 us
  waiting for transfers between devices: 12.4 us -> 3.6 us
  starting transfers between devices: 14.1 us -> 6.02 us
  Pallas kernels: 8.48 us -> 6.01 us
  local copies, waits for them, and re-layouts: 2.05 us -> 0.01 us
  other arithmetic: 2.27 us -> 1.29 us
    all_to_all x1 -> x2, blocking collectives: 11.3 us -> 27.3 us  [shared(): return lax.all_to_all(copies, axes, 0, 0, tiled=True)]
    all_to_all x1 -> x0, starting transfers between devices: 8.17 us -> none  [shared(): lax.all_to_all(jnp.broadcast_to(x, (n, *x.shape)), axes, 0, 0, tiled=True)]
    all_to_all x1 -> x0, waiting for transfers between devices: 7.4 us -> none  [shared(): lax.all_to_all(jnp.broadcast_to(x, (n, *x.shape)), axes, 0, 0, tiled=True)]
    pallas_call x3, Pallas kernels: 8.48 us -> 6.01 us  [the longest x1 3.81 us: shards(): pl.pallas_call(stats_kernel, in_specs=[pl.BlockSpec(memory_space=pl.ANY),...]
    ppermute x2, waiting for transfers between devices: 5.04 us -> 3.6 us  [swapped(): return lax.ppermute(x, axis, [(0, 1), (1, 0)])]
    broadcast_in_dim x2 -> x1, local copies, waits for them, and re-layouts: 1.39 us -> 0.01 us  [shards(): jnp.broadcast_to(part, (lax.axis_size(far), *part.shape))]
    add x1, other arithmetic: 0.93 us -> 0.02 us  [shards(): sums = sums + swapped(sums, 'core')]
    unnamed x6 -> x0, local copies, waits for them, and re-layouts: 0.66 us -> none
  transfers between devices with their start and end apart: 3 -> 2, of which waited for: 3 -> 2; matrix products, arithmetic and copies ran while one was open for 1% -> 3% of each run, Pallas kernels for 0% -> 0%
where the time goes in v2:
time: 45.2 us; the launch traced here: 44.9 us
  blocking collectives  27.3 us (60%)
  starting transfers between devices  6.02 us (13%)
  Pallas kernels  6.01 us (13%)
  waiting for transfers between devices  3.6 us (8%)
  other arithmetic  1.29 us (3%)
  between operations  0.68 us (2%)
    all_to_all x2, blocking collectives, shared(): return lax.all_to_all(copies, axes, 0, 0, tiled=True)  27.3 us
    ppermute x2, starting transfers between devices, swapped(): return lax.ppermute(x, axis, [(0, 1), (1, 0)])  6.02 us
    pallas_call x1, Pallas kernels, shards(): pl.pallas_call(stats_kernel, in_specs=[pl.BlockSpec(memory_space=pl.ANY),...  3.81 us
    ppermute x2, waiting for transfers between devices, swapped(): return lax.ppermute(x, axis, [(0, 1), (1, 0)])  3.6 us
    pallas_call x1, Pallas kernels, shards(): pl.pallas_call(accumulate_kernel, in_specs=[whole, whole, whole, whole],...  1.42 us
  transfers between devices with their start and end apart: 2, of which 2 were waited for; matrix products, arithmetic and copies ran while one was open for 3% of the time, Pallas kernels for 0%

profile of v2, /device:TPU:1, one launch (start us, length us, event | category | flops | bytes accessed | tf_op | source)
XLA Modules:
  0.0 44.9 jit_solution(4749655721499965187)
XLA Ops:
  0.6 3.8 %shard_map.58 = (f32[8,32,128]{2,1,0:T(8,128)S(1)}, bf16[4096,128]{1,0:T(8,128)(2,1)S(1)}, bf16[256,128]{1,0:T(8,128)(2,1)S(1)}, f32[256,128]{1,0:T(8,128)S(1)}) custom-call(bf16[4096,128]{1,0:T(8,128)(2,1)} %samples_hbm.1, bf16[256,128]{1,0:T(8,128)(2,1)} %centres_ref.1, f32[2,128]{1,0:T(2,128)} %bitcast.4), custom_call_target="tpu_custom_call" | custom-call | tf_op jit(solution)/shard_map/pallas_call | solution.py:132
  4.4 11.3 %all_to_all.10 = f32[8,32,128]{2,1,0:T(8,128)S(1)} all-to-all(f32[8,32,128]{2,1,0:T(8,128)S(1)} %get-tuple-element.14), channel_id=1, replica_groups=mesh['xh'=2,'core'=2,'z'=8,'y'=4,'xl'=2] {'y','xl'}, dimensions={0} | all-to-all | bytes 262144 | tf_op jit(solution)/shard_map/all_to_all | solution.py:109
  15.8 16.0 %all_to_all.11.parts_ref = f32[8,32,128]{2,1,0:T(8,128)S(1)} all-to-all(f32[8,32,128]{2,1,0:T(8,128)S(1)} %broadcast_in_dim.4), channel_id=1, replica_groups=mesh['xh'=2,'core'=2,'z'=8,'y'=4,'xl'=2] {'z'}, dimensions={0} | all-to-all | bytes 262144 | tf_op jit(solution)/shard_map/all_to_all | solution.py:109
  31.9 1.4 %shard_map.59 = (f32[264,128]{1,0:T(8,128)S(1)}, f32[32,128]{1,0:T(8,128)S(1)}) custom-call(bf16[4096,128]{1,0:T(8,128)(2,1)S(1)} %get-tuple-element.11.samples_ref, bf16[256,128]{1,0:T(8,128)(2,1)S(1)} %get-tuple-element.12.centres_ref.refs_2_, f32[256,128]{1,0:T(8,128)S(1)} %get-tuple-element.13.bias_ref, f32[8,32,128]{2,1,0:T(8,128)S(1)} %all_to_all.11.parts_ref), custom_call_target="tpu_custom_call" | custom-call | tf_op jit(solution)/shard_map/pallas_call | solution.py:146
  33.3 3.5 %collective-permute-start = (f32[264,128]{1,0:T(8,128)S(1)}, f32[264,128]{1,0:T(8,128)S(1)}, u32[]{:S(2)}, u32[]{:S(2)}) collective-permute-start(f32[264,128]{1,0:T(8,128)S(1)} %get-tuple-element.15), channel_id=1, source_target_pairs={{0,64},{64,0},{1,65},{65,1},{2,66},{66,2},{3,67},{67,3},{4,68},{68... | collective-permute-start | bytes 405512 | tf_op jit(solution)/shard_map/ppermute | solution.py:122
  36.8 0.6 %multiply_reduce_fusion = f32[4096]{0:T(1024)S(1)} fusion(bf16[4096,128]{1,0:T(8,128)(2,1)S(1)} %get-tuple-element.11.samples_ref), kind=kLoop, calls=%fused_computation | loop fusion | flops 1568768 | bytes 1064960 | tf_op jit(solution)/shard_map/reduce_sum | solution.py:158
  37.4 0.4 collective-permute-done
  37.8 2.5 %collective-permute-start.1 = (f32[264,128]{1,0:T(8,128)S(1)}, f32[264,128]{1,0:T(8,128)S(1)}, u32[]{:S(2)}, u32[]{:S(2)}) collective-permute-start(f32[264,128]{1,0:T(8,128)S(1)} %add.7.refs_0_), channel_id=1, source_target_pairs={{0,128},{128,0},{1,129},{129,1},{2,130},{130,2},{3,131},{131,3},{4... | collective-permute-start | bytes 405512 | tf_op jit(solution)/shard_map/ppermute | solution.py:122
  40.3 0.6 %bitcast_subtract_fusion = f32[4096]{0:T(1024)} fusion(f32[4096]{0:T(1024)S(1)} %multiply_reduce_fusion, f32[32,128]{1,0:T(8,128)S(1)} %get-tuple-element.18), kind=kLoop, calls=%fused_computation.2 | loop fusion | flops 12288 | bytes 49152 | tf_op jit(solution)/shard_map/sub | solution.py:159
  40.9 3.2 %collective-permute-done.1.refs_1_ = f32[264,128]{1,0:T(8,128)S(1)} collective-permute-done((f32[264,128]{1,0:T(8,128)S(1)}, f32[264,128]{1,0:T(8,128)S(1)}, u32[]{:S(2)}, u32[]{:S(2)}) %collective-permute-start.1) | collective-permute-done | bytes 135200 | tf_op jit(solution)/shard_map/ppermute | solution.py:122
  44.2 0.8 %shard_map.60 = (f32[256,128]{1,0:T(8,128)}, f32[2,128]{1,0:T(2,128)}) custom-call(f32[264,128]{1,0:T(8,128)S(1)} %add.7.refs_0_, f32[264,128]{1,0:T(8,128)S(1)} %collective-permute-done.1.refs_1_, bf16[256,128]{1,0:T(8,128)(2,1)S(1)} %get-tuple-element.12.centres_ref.refs_2_), custom_call_target="tpu_custom_call" | custom-call | tf_op jit(solution)/shard_map/pallas_call | solution.py:161
  (5 shorter events, 0.1 us)
Async XLA Ops:
  33.3 4.5 %collective-permute-start = (f32[264,128]{1,0:T(8,128)S(1)}, f32[264,128]{1,0:T(8,128)S(1)}, u32[]{:S(2)}, u32[]{:S(2)}) collective-permute-start(f32[264,128]{1,0:T(8,128)S(1)} %get-tuple-element.15), channel_id=1, source_target_pairs={{0,64},{64,0},{1,65},{65,1},{2,66},{66,2},{3,67},{67,3},{4,68},{68... | collective-permute-start | bytes 405512 | tf_op jit(solution)/shard_map/ppermute | solution.py:122
  37.8 6.4 %collective-permute-start.1 = (f32[264,128]{1,0:T(8,128)S(1)}, f32[264,128]{1,0:T(8,128)S(1)}, u32[]{:S(2)}, u32[]{:S(2)}) collective-permute-start(f32[264,128]{1,0:T(8,128)S(1)} %add.7.refs_0_), channel_id=1, source_target_pairs={{0,128},{128,0},{1,129},{129,1},{2,130},{130,2},{3,131},{131,3},{4... | collective-permute-start | bytes 405512 | tf_op jit(solution)/shard_map/ppermute | solution.py:122

commit v3 on v2

v3 whole, which is shorter than its diff:
```python
import jax
import jax.numpy as jnp
import numpy as np
from jax import lax
from jax.experimental import pallas as pl
from jax.experimental.pallas import tpu as pltpu
from jax.sharding import Mesh
from jax.sharding import PartitionSpec as P


AXES = ("xh", "core", "z", "y", "xl")
DP = ("xh", "core")
CENTRE = ("z", "y", "xl")

inverse_coolness_beta = 0.0625
LOG2E = float(np.log2(np.e))
LN2 = float(np.log(2.0))
CROSS2 = 2.0 * inverse_coolness_beta * LOG2E

LANES = 128
TILE = 256
CHUNKS = 2
SMALL = pltpu.CompilerParams(vmem_limit_bytes=16 << 20)


def column_of(row):
    return jnp.transpose(jnp.broadcast_to(row, (LANES, LANES)))


def centre_bias(centres_ref, prior_ref):
    wide = centres_ref[...].astype(jnp.float32)
    norm = jnp.sum(wide * wide, axis=1, keepdims=True)
    prior = jnp.concatenate([column_of(prior_ref[k : k + 1, :]) for k in range(prior_ref.shape[0])])
    return (prior - norm * inverse_coolness_beta) * LOG2E


def stats_kernel(
    samples_hbm, centres_hbm, prior_hbm, out_ref, samples_ref, centres_ref, scaled_ref, top_ref, prior_ref, sems
):
    pairs = [(centres_hbm, centres_ref), (prior_hbm, prior_ref)]
    step = samples_ref.shape[0] // CHUNKS
    for k in range(CHUNKS):
        rows = pl.ds(k * step, step)
        pairs.append((samples_hbm.at[rows, :], samples_ref.at[rows, :]))
    copies = [pltpu.make_async_copy(a, b, sems.at[k]) for k, (a, b) in enumerate(pairs)]
    for copy in copies:
        copy.start()
    copies[0].wait()
    copies[1].wait()
    bias = centre_bias(centres_ref, prior_ref)
    for t in range(samples_ref.shape[0] // TILE):
        if t * TILE % step == 0:
            copies[2 + t * TILE // step].wait()
        cross = lax.dot_general(
            centres_ref[...],
            samples_ref[t * TILE : (t + 1) * TILE, :],
            (((1,), (1,)), ((), ())),
            preferred_element_type=jnp.float32,
        )
        for h in range(TILE // LANES):
            at = t * (TILE // LANES) + h
            score = cross[:, h * LANES : (h + 1) * LANES] * CROSS2 + bias
            top = jnp.max(score, axis=0, keepdims=True)
            scaled = jnp.exp2(score - top)
            scaled_ref[:, at * LANES : (at + 1) * LANES] = scaled
            total = jnp.sum(scaled, axis=0, keepdims=True)
            top_ref[at : at + 1, :] = top
            out_ref[0, at : at + 1, :] = top + jnp.log2(total)
    for k in range(1, out_ref.shape[0]):
        out_ref[k, :, :] = out_ref[0, :, :]


def merge_kernel(parts_ref, out_ref):
    part = merged(parts_ref[...])
    for k in range(out_ref.shape[0]):
        out_ref[k, :, :] = part


def accumulate_kernel(samples_ref, scaled_ref, top_ref, parts_ref, out_ref, partition_ref, factor_ref):
    partition = merged(parts_ref[...])
    partition_ref[...] = partition
    factor_ref[...] = jnp.exp2(top_ref[...] - partition)
    local = scaled_ref.shape[0]
    sums = jnp.zeros((local, 2 * LANES), jnp.float32)
    ones = jnp.ones((TILE, LANES), jnp.bfloat16)
    for t in range(samples_ref.shape[0] // TILE):
        resp = []
        for h in range(TILE // LANES):
            at = t * (TILE // LANES) + h
            scaled = scaled_ref[:, at * LANES : (at + 1) * LANES]
            resp.append((scaled * factor_ref[at : at + 1, :]).astype(jnp.bfloat16))
        rows = samples_ref[t * TILE : (t + 1) * TILE, :]
        sums = sums + lax.dot_general(
            jnp.concatenate(resp, axis=1),
            jnp.concatenate([rows, ones], axis=1),
            (((1,), (0,)), ((), ())),
            preferred_element_type=jnp.float32,
        )
    out_ref[0:local, :] = sums[:, :LANES]
    out_ref[local:, :] = jnp.zeros((out_ref.shape[0] - local, LANES), jnp.float32)
    for k in range(local // LANES):
        block = jnp.transpose(sums[k * LANES : (k + 1) * LANES, LANES:])
        out_ref[local + k : local + k + 1, :] = block[0:1, :]


def finish_kernel(denominator, mine_ref, other_ref, centres_ref, new_ref, prior_ref):
    local = centres_ref.shape[0]
    for k in range(local // LANES):
        rows = slice(k * LANES, (k + 1) * LANES)
        at = slice(local + k, local + k + 1)
        mass = mine_ref[at, :] + other_ref[at, :] + 1.0
        prior_ref[k : k + 1, :] = jnp.log(mass / denominator)
        weighted = mine_ref[rows, :] + other_ref[rows, :]
        new_ref[rows, :] = (weighted + centres_ref[rows, :].astype(jnp.float32)) / column_of(mass)


def shared(copies, axes):
    return lax.all_to_all(copies, axes, 0, 0, tiled=True)


def on_chip(x):
    return pltpu.with_memory_space_constraint(x, pltpu.VMEM)


def merged(parts):
    top = jnp.max(parts, axis=0)
    return top + jnp.log2(jnp.sum(jnp.exp2(parts - top), axis=0))


def swapped(x, axis):
    return lax.ppermute(x, axis, [(0, 1), (1, 0)])


def shards(samples, centres, facility_prior_logprob):
    rows, features = samples.shape
    local = centres.shape[0]
    prior = facility_prior_logprob.reshape(local // LANES, LANES)
    lines = rows // LANES
    near, far = ("y", "xl"), "z"
    whole = pl.BlockSpec(memory_space=pltpu.VMEM)
    anywhere = pl.BlockSpec(memory_space=pl.ANY)
    copies, samples_here, centres_here, scaled, top = pl.pallas_call(
        stats_kernel,
        in_specs=[anywhere] * 3,
        out_specs=[whole] * 5,
        out_shape=(
            pltpu.VMEM((lax.axis_size(near), lines, LANES), jnp.float32),
            pltpu.VMEM((rows, features), samples.dtype),
            pltpu.VMEM((local, features), centres.dtype),
            pltpu.VMEM((local, rows), jnp.float32),
            pltpu.VMEM((lines, LANES), jnp.float32),
        ),
        compiler_params=SMALL,
        scratch_shapes=[
            pltpu.VMEM(prior.shape, jnp.float32),
            pltpu.SemaphoreType.DMA((CHUNKS + 2,)),
        ],
    )(samples, centres, prior)
    copies = pl.pallas_call(
        merge_kernel,
        in_specs=[whole],
        out_specs=whole,
        out_shape=pltpu.VMEM((lax.axis_size(far), lines, LANES), jnp.float32),
        compiler_params=SMALL,
    )(on_chip(shared(copies, near)))
    parts = shared(copies, far)
    sums, partition = pl.pallas_call(
        accumulate_kernel,
        in_specs=[whole] * 4,
        out_specs=[whole, whole],
        out_shape=(
            pltpu.VMEM((local + 8, features), jnp.float32),
            pltpu.VMEM((lines, LANES), jnp.float32),
        ),
        compiler_params=SMALL,
        scratch_shapes=[pltpu.VMEM((lines, LANES), jnp.float32)],
    )(on_chip(samples_here), on_chip(scaled), on_chip(top), on_chip(parts))
    other = swapped(sums, "xh")
    wide = samples_here.astype(jnp.float32)
    norms = jnp.sum(wide * wide, axis=1)
    log_partition = partition.reshape(rows) * LN2 - norms * inverse_coolness_beta
    sums = sums + other
    other = swapped(sums, "core")
    denominator = float(rows * lax.axis_size(DP) + local * lax.axis_size(CENTRE))
    new_centres, new_log_prior = pl.pallas_call(
        lambda *refs: finish_kernel(denominator, *refs),
        in_specs=[whole, whole, whole],
        out_shape=(
            jax.ShapeDtypeStruct((local, features), jnp.float32),
            jax.ShapeDtypeStruct((local // LANES, LANES), jnp.float32),
        ),
    )(on_chip(sums), on_chip(other), on_chip(centres_here))
    return new_centres, new_log_prior.reshape(local), log_partition


def solution(mesh):
    torus = Mesh(mesh.devices.reshape(2, 2, 8, 4, 2), AXES)
    in_specs = (P(DP, None), P(CENTRE, None), P(CENTRE))
    out_specs = (P(CENTRE, None), P(CENTRE), P(DP))
    return jax.shard_map(
        shards, mesh=torus, in_specs=in_specs, out_specs=out_specs, check_vma=False
    )
```

time: 45.2 us -> 45.7 us (1.011)
  local copies, waits for them, and re-layouts: 0.01 us -> 2.74 us
  Pallas kernels: 6.01 us -> 3.63 us
  starting transfers between devices: 6.02 us -> 7.15 us
  waiting for transfers between devices: 3.6 us -> 2.68 us
    unnamed x0 -> x6, local copies, waits for them, and re-layouts: none -> 2.74 us
    pallas_call x2 -> x3, Pallas kernels: 5.23 us -> 2.86 us  [the longest x1 2.04 us: shards(): pl.pallas_call(stats_kernel, in_specs=[anywhere] * 3, out_specs=[whole] *...]
    ppermute x2, starting transfers between devices: 6.02 us -> 7.15 us  [swapped(): return lax.ppermute(x, axis, [(0, 1), (1, 0)])]
    ppermute x2, waiting for transfers between devices: 3.6 us -> 2.68 us  [swapped(): return lax.ppermute(x, axis, [(0, 1), (1, 0)])]
where the time goes in v3:
time: 45.7 us; the launch traced here: 45.4 us
  blocking collectives  27.3 us (60%)
  starting transfers between devices  7.15 us (16%)
  Pallas kernels  3.63 us (8%)
  local copies, waits for them, and re-layouts  2.74 us (6%)
  waiting for transfers between devices  2.68 us (6%)
  other arithmetic  1.24 us (3%)
  between operations  0.67 us (1%)
    all_to_all x2, blocking collectives, shared(): return lax.all_to_all(copies, axes, 0, 0, tiled=True)  27.3 us
    ppermute x2, starting transfers between devices, swapped(): return lax.ppermute(x, axis, [(0, 1), (1, 0)])  7.15 us
    unnamed x6, local copies, waits for them, and re-layouts  2.74 us
    ppermute x2, waiting for transfers between devices, swapped(): return lax.ppermute(x, axis, [(0, 1), (1, 0)])  2.68 us
    pallas_call x1, Pallas kernels, shards(): pl.pallas_call(stats_kernel, in_specs=[anywhere] * 3, out_specs=[whole] *...  2.04 us
  transfers between devices with their start and end apart: 2, of which 2 were waited for; matrix products, arithmetic and copies ran while one was open for 3% of the time, Pallas kernels for 0%

profile of v3, /device:TPU:1, one launch (start us, length us, event | category | flops | bytes accessed | tf_op | source)
XLA Modules:
  0.0 45.4 jit_solution(9908077147746276608)
XLA Ops:
  0.6 0.0 copy-start
  0.6 1.2 %copy-done = bf16[4096,128]{1,0:T(8,128)(2,1)S(1)} copy-done((bf16[4096,128]{1,0:T(8,128)(2,1)S(1)}, bf16[4096,128]{1,0:T(8,128)(2,1)}, u32[]{:S(2)}) %copy-start) | copy-done | bytes 1048600
  1.9 0.0 copy-start.1
  1.9 0.8 %copy-done.1 = bf16[256,128]{1,0:T(8,128)(2,1)S(1)} copy-done((bf16[256,128]{1,0:T(8,128)(2,1)S(1)}, bf16[256,128]{1,0:T(8,128)(2,1)}, u32[]{:S(2)}) %copy-start.1) | copy-done | bytes 65560
  2.7 0.0 copy-start.2
  2.7 0.7 %copy-done.2 = f32[256]{0:T(256)S(1)} copy-done((f32[256]{0:T(256)S(1)}, f32[256]{0:T(256)}, u32[]{:S(2)}) %copy-start.2) | copy-done | bytes 1048
  3.4 2.0 %shard_map.58 = (f32[8,32,128]{2,1,0:T(8,128)S(1)}, bf16[4096,128]{1,0:T(8,128)(2,1)S(1)}, bf16[256,128]{1,0:T(8,128)(2,1)S(1)}, f32[256,4096]{1,0:T(8,128)S(1)}, f32[32,128]{1,0:T(8,128)S(1)}) custom-call(bf16[4096,128]{1,0:T(8,128)(2,1)S(1)} %copy-done, bf16[256,128]{1,0:T(8,128)(2,1)S(1)} %copy-done.1, f32[2,128]{1,0:T(2,128)S(1)} %bitcast.4), custom_call_target="tpu_custom_call" | custom-call | tf_op jit(solution)/shard_map/pallas_call | solution.py:142
  5.4 11.3 %all_to_all.10.parts_ref = f32[8,32,128]{2,1,0:T(8,128)S(1)} all-to-all(f32[8,32,128]{2,1,0:T(8,128)S(1)} %get-tuple-element.15), channel_id=1, replica_groups=mesh['xh'=2,'core'=2,'z'=8,'y'=4,'xl'=2] {'y','xl'}, dimensions={0} | all-to-all | bytes 262144 | tf_op jit(solution)/shard_map/all_to_all | solution.py:118
  16.8 16.0 %all_to_all.11.parts_ref = f32[8,32,128]{2,1,0:T(8,128)S(1)} all-to-all(f32[8,32,128]{2,1,0:T(8,128)S(1)} %shard_map.59), channel_id=1, replica_groups=mesh['xh'=2,'core'=2,'z'=8,'y'=4,'xl'=2] {'z'}, dimensions={0} | all-to-all | bytes 262144 | tf_op jit(solution)/shard_map/all_to_all | solution.py:118
  32.8 0.8 %shard_map.60 = (f32[264,128]{1,0:T(8,128)S(1)}, f32[32,128]{1,0:T(8,128)S(1)}) custom-call(bf16[4096,128]{1,0:T(8,128)(2,1)S(1)} %get-tuple-element.12.samples_ref, f32[256,4096]{1,0:T(8,128)S(1)} %get-tuple-element.13.scaled_ref, f32[32,128]{1,0:T(8,128)S(1)} %get-tuple-element.14.top_ref, f32[8,32,128]{2,1,0:T(8,128)S(1)} %all_to_all.11.parts_ref), custom_call_target="tpu_custom_call" | custom-call | tf_op jit(solution)/shard_map/pallas_call | solution.py:167
  33.6 2.5 %collective-permute-start = (f32[264,128]{1,0:T(8,128)S(1)}, f32[264,128]{1,0:T(8,128)S(1)}, u32[]{:S(2)}, u32[]{:S(2)}) collective-permute-start(f32[264,128]{1,0:T(8,128)S(1)} %get-tuple-element.16), channel_id=1, source_target_pairs={{0,128},{128,0},{1,129},{129,1},{2,130},{130,2},{3,131},{131,3},{4... | collective-permute-start | bytes 405512 | tf_op jit(solution)/shard_map/ppermute | solution.py:131
  36.1 0.6 %multiply_reduce_fusion = f32[4096]{0:T(1024)S(1)} fusion(bf16[4096,128]{1,0:T(8,128)(2,1)S(1)} %get-tuple-element.12.samples_ref), kind=kLoop, calls=%fused_computation | loop fusion | flops 1568768 | bytes 1064960 | tf_op jit(solution)/shard_map/reduce_sum | solution.py:180
  36.7 2.3 %collective-permute-done = f32[264,128]{1,0:T(8,128)S(1)} collective-permute-done((f32[264,128]{1,0:T(8,128)S(1)}, f32[264,128]{1,0:T(8,128)S(1)}, u32[]{:S(2)}, u32[]{:S(2)}) %collective-permute-start) | collective-permute-done | bytes 135200 | tf_op jit(solution)/shard_map/ppermute | solution.py:131
  39.0 4.6 %collective-permute-start.1 = (f32[264,128]{1,0:T(8,128)S(1)}, f32[264,128]{1,0:T(8,128)S(1)}, u32[]{:S(2)}, u32[]{:S(2)}) collective-permute-start(f32[264,128]{1,0:T(8,128)S(1)} %add.3.refs_0_), channel_id=1, source_target_pairs={{0,64},{64,0},{1,65},{65,1},{2,66},{66,2},{3,67},{67,3},{4,68},{68... | collective-permute-start | bytes 405512 | tf_op jit(solution)/shard_map/ppermute | solution.py:131
  43.7 0.6 %bitcast_subtract_fusion = f32[4096]{0:T(1024)} fusion(f32[4096]{0:T(1024)S(1)} %multiply_reduce_fusion, f32[32,128]{1,0:T(8,128)S(1)} %get-tuple-element.20), kind=kLoop, calls=%fused_computation.1 | loop fusion | flops 12288 | bytes 49152 | tf_op jit(solution)/shard_map/sub | solution.py:181
  44.3 0.4 collective-permute-done.1.refs_1_
  44.6 0.8 %shard_map.61 = (f32[256,128]{1,0:T(8,128)}, f32[2,128]{1,0:T(2,128)}) custom-call(f32[264,128]{1,0:T(8,128)S(1)} %add.3.refs_0_, f32[264,128]{1,0:T(8,128)S(1)} %collective-permute-done.1.refs_1_, bf16[256,128]{1,0:T(8,128)(2,1)S(1)} %get-tuple-element.17.refs_2_), custom_call_target="tpu_custom_call" | custom-call | tf_op jit(solution)/shard_map/pallas_call | solution.py:185
  (2 shorter events, 0.1 us)
Async XLA Ops:
  0.6 1.2 %copy-start = (bf16[4096,128]{1,0:T(8,128)(2,1)S(1)}, bf16[4096,128]{1,0:T(8,128)(2,1)}, u32[]{:S(2)}) copy-start(bf16[4096,128]{1,0:T(8,128)(2,1)} %samples_hbm.1) | copy-start | bytes 3145732
  1.9 0.8 %copy-start.1 = (bf16[256,128]{1,0:T(8,128)(2,1)S(1)}, bf16[256,128]{1,0:T(8,128)(2,1)}, u32[]{:S(2)}) copy-start(bf16[256,128]{1,0:T(8,128)(2,1)} %centres_hbm.1) | copy-start | bytes 196612
  2.7 0.7 %copy-start.2 = (f32[256]{0:T(256)S(1)}, f32[256]{0:T(256)}, u32[]{:S(2)}) copy-start(f32[256]{0:T(256)} %param.5) | copy-start | bytes 3076
  33.6 5.4 %collective-permute-start = (f32[264,128]{1,0:T(8,128)S(1)}, f32[264,128]{1,0:T(8,128)S(1)}, u32[]{:S(2)}, u32[]{:S(2)}) collective-permute-start(f32[264,128]{1,0:T(8,128)S(1)} %get-tuple-element.16), channel_id=1, source_target_pairs={{0,128},{128,0},{1,129},{129,1},{2,130},{130,2},{3,131},{131,3},{4... | collective-permute-start | bytes 405512 | tf_op jit(solution)/shard_map/ppermute | solution.py:131
  39.0 5.6 %collective-permute-start.1 = (f32[264,128]{1,0:T(8,128)S(1)}, f32[264,128]{1,0:T(8,128)S(1)}, u32[]{:S(2)}, u32[]{:S(2)}) collective-permute-start(f32[264,128]{1,0:T(8,128)S(1)} %add.3.refs_0_), channel_id=1, source_target_pairs={{0,64},{64,0},{1,65},{65,1},{2,66},{66,2},{3,67},{67,3},{4,68},{68... | collective-permute-start | bytes 405512 | tf_op jit(solution)/shard_map/ppermute | solution.py:131

commit v4 on v3

--- a/solution.py
+++ b/solution.py
@@ -19,7 +19,7 @@
 
 LANES = 128
 TILE = 256
-CHUNKS = 2
+CHUNKS = 4
 SMALL = pltpu.CompilerParams(vmem_limit_bytes=16 << 20)
 
 
@@ -27,11 +27,18 @@
     return jnp.transpose(jnp.broadcast_to(row, (LANES, LANES)))
 
 
-def centre_bias(centres_ref, prior_ref):
+def bias_parts(centres_ref, prior_ref):
     wide = centres_ref[...].astype(jnp.float32)
     norm = jnp.sum(wide * wide, axis=1, keepdims=True)
     prior = jnp.concatenate([column_of(prior_ref[k : k + 1, :]) for k in range(prior_ref.shape[0])])
-    return (prior - norm * inverse_coolness_beta) * LOG2E
+    rest = prior * (0.5 / inverse_coolness_beta) - norm * 0.5
+    lane = lax.broadcasted_iota(jnp.int32, rest.shape, 1)
+    parts = jnp.zeros(rest.shape, jnp.float32)
+    for k in range(3):
+        part = rest.astype(jnp.bfloat16).astype(jnp.float32)
+        parts = jnp.where(lane == k, part, parts)
+        rest = rest - part
+    return parts.astype(jnp.bfloat16)
 
 
 def stats_kernel(
@@ -47,25 +54,36 @@
         copy.start()
     copies[0].wait()
     copies[1].wait()
-    bias = centre_bias(centres_ref, prior_ref)
-    for t in range(samples_ref.shape[0] // TILE):
-        if t * TILE % step == 0:
-            copies[2 + t * TILE // step].wait()
-        cross = lax.dot_general(
-            centres_ref[...],
-            samples_ref[t * TILE : (t + 1) * TILE, :],
+    extended = jnp.concatenate([centres_ref[...], bias_parts(centres_ref, prior_ref)], axis=1)
+    ones = jnp.ones((TILE, LANES), jnp.bfloat16)
+
+    def scores(t):
+        rows = samples_ref[pl.ds(t * TILE, TILE), :]
+        return lax.dot_general(
+            extended,
+            jnp.concatenate([rows, ones], axis=1),
             (((1,), (1,)), ((), ())),
             preferred_element_type=jnp.float32,
         )
+
+    def reduce(t, score):
         for h in range(TILE // LANES):
             at = t * (TILE // LANES) + h
-            score = cross[:, h * LANES : (h + 1) * LANES] * CROSS2 + bias
-            top = jnp.max(score, axis=0, keepdims=True)
-            scaled = jnp.exp2(score - top)
-            scaled_ref[:, at * LANES : (at + 1) * LANES] = scaled
+            half = score[:, h * LANES : (h + 1) * LANES]
+            top = jnp.max(half, axis=0, keepdims=True)
+            scaled = jnp.exp2((half - top) * CROSS2)
+            scaled_ref[at, :, :] = scaled
             total = jnp.sum(scaled, axis=0, keepdims=True)
-            top_ref[at : at + 1, :] = top
-            out_ref[0, at : at + 1, :] = top + jnp.log2(total)
+            top_ref[pl.ds(at, 1), :] = top * CROSS2
+            out_ref[0, pl.ds(at, 1), :] = top * CROSS2 + jnp.log2(total)
+
+    for copy in copies[2:]:
+        copy.wait()
+    tiles = samples_ref.shape[0] // TILE
+    ahead = scores(0)
+    for t in range(tiles):
+        score, ahead = ahead, scores(min(t + 1, tiles - 1))
+        reduce(t, score)
     for k in range(1, out_ref.shape[0]):
         out_ref[k, :, :] = out_ref[0, :, :]
 
@@ -80,14 +98,14 @@
     partition = merged(parts_ref[...])
     partition_ref[...] = partition
     factor_ref[...] = jnp.exp2(top_ref[...] - partition)
-    local = scaled_ref.shape[0]
+    local = scaled_ref.shape[1]
     sums = jnp.zeros((local, 2 * LANES), jnp.float32)
     ones = jnp.ones((TILE, LANES), jnp.bfloat16)
     for t in range(samples_ref.shape[0] // TILE):
         resp = []
         for h in range(TILE // LANES):
             at = t * (TILE // LANES) + h
-            scaled = scaled_ref[:, at * LANES : (at + 1) * LANES]
+            scaled = scaled_ref[at]
             resp.append((scaled * factor_ref[at : at + 1, :]).astype(jnp.bfloat16))
         rows = samples_ref[t * TILE : (t + 1) * TILE, :]
         sums = sums + lax.dot_general(
@@ -122,6 +140,10 @@
     return pltpu.with_memory_space_constraint(x, pltpu.VMEM)
 
 
+def in_hbm(x):
+    return pltpu.with_memory_space_constraint(x, pltpu.HBM)
+
+
 def merged(parts):
     top = jnp.max(parts, axis=0)
     return top + jnp.log2(jnp.sum(jnp.exp2(parts - top), axis=0))
@@ -138,16 +160,15 @@
     lines = rows // LANES
     near, far = ("y", "xl"), "z"
     whole = pl.BlockSpec(memory_space=pltpu.VMEM)
-    anywhere = pl.BlockSpec(memory_space=pl.ANY)
     copies, samples_here, centres_here, scaled, top = pl.pallas_call(
         stats_kernel,
-        in_specs=[anywhere] * 3,
+        in_specs=[pl.BlockSpec(memory_space=pltpu.HBM)] * 3,
         out_specs=[whole] * 5,
         out_shape=(
             pltpu.VMEM((lax.axis_size(near), lines, LANES), jnp.float32),
             pltpu.VMEM((rows, features), samples.dtype),
             pltpu.VMEM((local, features), centres.dtype),
-            pltpu.VMEM((local, rows), jnp.float32),
+            pltpu.VMEM((lines, local, LANES), jnp.float32),
             pltpu.VMEM((lines, LANES), jnp.float32),
         ),
         compiler_params=SMALL,
@@ -155,7 +176,7 @@
             pltpu.VMEM(prior.shape, jnp.float32),
             pltpu.SemaphoreType.DMA((CHUNKS + 2,)),
         ],
-    )(samples, centres, prior)
+    )(in_hbm(samples), in_hbm(centres), in_hbm(prior))
     copies = pl.pallas_call(
         merge_kernel,
         in_specs=[whole],

time: 45.7 us -> 43.5 us (0.952)
  local copies, waits for them, and re-layouts: 2.74 us -> 0 us
  Pallas kernels: 3.63 us -> 4.24 us
    unnamed x6 -> x0, local copies, waits for them, and re-layouts: 2.74 us -> none
    pallas_call x1, Pallas kernels: 2.04 us -> 2.65 us  [shards(): pl.pallas_call(stats_kernel, in_specs=[pl.BlockSpec(memory_space=pltpu.HB...]
where the time goes in v4:
time: 43.5 us; the launch traced here: 43.3 us
  blocking collectives  27.3 us (63%)
  starting transfers between devices  7.17 us (16%)
  Pallas kernels  4.24 us (10%)
  waiting for transfers between devices  2.67 us (6%)
  other arithmetic  1.24 us (3%)
  between operations  0.66 us (2%)
    all_to_all x2, blocking collectives, shared(): return lax.all_to_all(copies, axes, 0, 0, tiled=True)  27.3 us
    ppermute x2, starting transfers between devices, swapped(): return lax.ppermute(x, axis, [(0, 1), (1, 0)])  7.17 us
    ppermute x2, waiting for transfers between devices, swapped(): return lax.ppermute(x, axis, [(0, 1), (1, 0)])  2.67 us
    pallas_call x1, Pallas kernels, shards(): pl.pallas_call(stats_kernel, in_specs=[pl.BlockSpec(memory_space=pltpu.HB...  2.65 us
  transfers between devices with their start and end apart: 2, of which 2 were waited for; matrix products, arithmetic and copies ran while one was open for 3% of the time, Pallas kernels for 0%

profile of v4, /device:TPU:1, one launch (start us, length us, event | category | flops | bytes accessed | tf_op | source)
XLA Modules:
  0.0 43.3 jit_solution(3456581904565880397)
XLA Ops:
  0.6 2.6 %shard_map.58 = (f32[8,32,128]{2,1,0:T(8,128)S(1)}, bf16[4096,128]{1,0:T(8,128)(2,1)S(1)}, bf16[256,128]{1,0:T(8,128)(2,1)S(1)}, f32[32,256,128]{2,1,0:T(8,128)S(1)}, f32[32,128]{1,0:T(8,128)S(1)}) custom-call(bf16[4096,128]{1,0:T(8,128)(2,1)} %samples_hbm.1, bf16[256,128]{1,0:T(8,128)(2,1)} %centres_hbm.1, f32[2,128]{1,0:T(2,128)} %bitcast.4), custom_call_target="tpu_custom_call" | custom-call | tf_op jit(solution)/shard_map/pallas_call | solution.py:163
  3.3 11.3 %all_to_all.10.parts_ref = f32[8,32,128]{2,1,0:T(8,128)S(1)} all-to-all(f32[8,32,128]{2,1,0:T(8,128)S(1)} %get-tuple-element.15), channel_id=1, replica_groups=mesh['xh'=2,'core'=2,'z'=8,'y'=4,'xl'=2] {'y','xl'}, dimensions={0} | all-to-all | bytes 262144 | tf_op jit(solution)/shard_map/all_to_all | solution.py:136
  14.6 16.0 %all_to_all.11.parts_ref = f32[8,32,128]{2,1,0:T(8,128)S(1)} all-to-all(f32[8,32,128]{2,1,0:T(8,128)S(1)} %shard_map.59), channel_id=1, replica_groups=mesh['xh'=2,'core'=2,'z'=8,'y'=4,'xl'=2] {'z'}, dimensions={0} | all-to-all | bytes 262144 | tf_op jit(solution)/shard_map/all_to_all | solution.py:136
  30.6 0.8 %shard_map.60 = (f32[264,128]{1,0:T(8,128)S(1)}, f32[32,128]{1,0:T(8,128)S(1)}) custom-call(bf16[4096,128]{1,0:T(8,128)(2,1)S(1)} %get-tuple-element.12.samples_ref, f32[32,256,128]{2,1,0:T(8,128)S(1)} %get-tuple-element.13.scaled_ref, f32[32,128]{1,0:T(8,128)S(1)} %get-tuple-element.14.top_ref, f32[8,32,128]{2,1,0:T(8,128)S(1)} %all_to_all.11.parts_ref), custom_call_target="tpu_custom_call" | custom-call | tf_op jit(solution)/shard_map/pallas_call | solution.py:188
  31.4 2.5 %collective-permute-start = (f32[264,128]{1,0:T(8,128)S(1)}, f32[264,128]{1,0:T(8,128)S(1)}, u32[]{:S(2)}, u32[]{:S(2)}) collective-permute-start(f32[264,128]{1,0:T(8,128)S(1)} %get-tuple-element.16), channel_id=1, source_target_pairs={{0,128},{128,0},{1,129},{129,1},{2,130},{130,2},{3,131},{131,3},{4... | collective-permute-start | bytes 405512 | tf_op jit(solution)/shard_map/ppermute | solution.py:153
  33.9 0.6 %multiply_reduce_fusion = f32[4096]{0:T(1024)S(1)} fusion(bf16[4096,128]{1,0:T(8,128)(2,1)S(1)} %get-tuple-element.12.samples_ref), kind=kLoop, calls=%fused_computation | loop fusion | flops 1568768 | bytes 1064960 | tf_op jit(solution)/shard_map/reduce_sum | solution.py:201
  34.6 2.3 %collective-permute-done = f32[264,128]{1,0:T(8,128)S(1)} collective-permute-done((f32[264,128]{1,0:T(8,128)S(1)}, f32[264,128]{1,0:T(8,128)S(1)}, u32[]{:S(2)}, u32[]{:S(2)}) %collective-permute-start) | collective-permute-done | bytes 135200 | tf_op jit(solution)/shard_map/ppermute | solution.py:153
  36.9 4.7 %collective-permute-start.1 = (f32[264,128]{1,0:T(8,128)S(1)}, f32[264,128]{1,0:T(8,128)S(1)}, u32[]{:S(2)}, u32[]{:S(2)}) collective-permute-start(f32[264,128]{1,0:T(8,128)S(1)} %add.3.refs_0_), channel_id=1, source_target_pairs={{0,64},{64,0},{1,65},{65,1},{2,66},{66,2},{3,67},{67,3},{4,68},{68... | collective-permute-start | bytes 405512 | tf_op jit(solution)/shard_map/ppermute | solution.py:153
  41.5 0.6 %bitcast_subtract_fusion = f32[4096]{0:T(1024)} fusion(f32[4096]{0:T(1024)S(1)} %multiply_reduce_fusion, f32[32,128]{1,0:T(8,128)S(1)} %get-tuple-element.20), kind=kLoop, calls=%fused_computation.1 | loop fusion | flops 12288 | bytes 49152 | tf_op jit(solution)/shard_map/sub | solution.py:202
  42.1 0.4 collective-permute-done.1.refs_1_
  42.5 0.8 %shard_map.61 = (f32[256,128]{1,0:T(8,128)}, f32[2,128]{1,0:T(2,128)}) custom-call(f32[264,128]{1,0:T(8,128)S(1)} %add.3.refs_0_, f32[264,128]{1,0:T(8,128)S(1)} %collective-permute-done.1.refs_1_, bf16[256,128]{1,0:T(8,128)(2,1)S(1)} %get-tuple-element.17.refs_2_), custom_call_target="tpu_custom_call" | custom-call | tf_op jit(solution)/shard_map/pallas_call | solution.py:206
  (2 shorter events, 0.1 us)
Async XLA Ops:
  31.4 5.4 %collective-permute-start = (f32[264,128]{1,0:T(8,128)S(1)}, f32[264,128]{1,0:T(8,128)S(1)}, u32[]{:S(2)}, u32[]{:S(2)}) collective-permute-start(f32[264,128]{1,0:T(8,128)S(1)} %get-tuple-element.16), channel_id=1, source_target_pairs={{0,128},{128,0},{1,129},{129,1},{2,130},{130,2},{3,131},{131,3},{4... | collective-permute-start | bytes 405512 | tf_op jit(solution)/shard_map/ppermute | solution.py:153
  36.9 5.7 %collective-permute-start.1 = (f32[264,128]{1,0:T(8,128)S(1)}, f32[264,128]{1,0:T(8,128)S(1)}, u32[]{:S(2)}, u32[]{:S(2)}) collective-permute-start(f32[264,128]{1,0:T(8,128)S(1)} %add.3.refs_0_), channel_id=1, source_target_pairs={{0,64},{64,0},{1,65},{65,1},{2,66},{66,2},{3,67},{67,3},{4,68},{68... | collective-permute-start | bytes 405512 | tf_op jit(solution)/shard_map/ppermute | solution.py:153

commit v5 on v4

--- a/solution.py
+++ b/solution.py
@@ -8,9 +8,10 @@
 from jax.sharding import PartitionSpec as P
 
 
-AXES = ("xh", "core", "z", "y", "xl")
+AXES = ("xh", "core", "z", "yx")
 DP = ("xh", "core")
-CENTRE = ("z", "y", "xl")
+CENTRE = ("z", "yx")
+MEMBERS = {"z": [4, 3, 2, 1, 5, 6, 7, 0], "yx": [5, 7, 6, 1, 4, 3, 2, 0]}
 
 inverse_coolness_beta = 0.0625
 LOG2E = float(np.log2(np.e))
@@ -132,8 +133,8 @@
         new_ref[rows, :] = (weighted + centres_ref[rows, :].astype(jnp.float32)) / column_of(mass)
 
 
-def shared(copies, axes):
-    return lax.all_to_all(copies, axes, 0, 0, tiled=True)
+def shared(copies, axis):
+    return lax.all_to_all(copies, axis, 0, 0, axis_index_groups=[MEMBERS[axis]], tiled=True)
 
 
 def on_chip(x):
@@ -158,7 +159,7 @@
     local = centres.shape[0]
     prior = facility_prior_logprob.reshape(local // LANES, LANES)
     lines = rows // LANES
-    near, far = ("y", "xl"), "z"
+    near, far = "yx", "z"
     whole = pl.BlockSpec(memory_space=pltpu.VMEM)
     copies, samples_here, centres_here, scaled, top = pl.pallas_call(
         stats_kernel,
@@ -215,7 +216,7 @@
 
 
 def solution(mesh):
-    torus = Mesh(mesh.devices.reshape(2, 2, 8, 4, 2), AXES)
+    torus = Mesh(mesh.devices.reshape(2, 2, 8, 8), AXES)
     in_specs = (P(DP, None), P(CENTRE, None), P(CENTRE))
     out_specs = (P(CENTRE, None), P(CENTRE), P(DP))
     return jax.shard_map(

time: 43.5 us -> 37.6 us (0.86)
  blocking collectives: 27.3 us -> 22.2 us
  starting transfers between devices: 7.17 us -> 6.42 us
    all_to_all x2, blocking collectives: 27.3 us -> 22.2 us  [shared(): lax.all_to_all(copies, axis, 0, 0, axis_index_groups=[MEMBERS[axis]], til...]
    ppermute x2, starting transfers between devices: 7.17 us -> 6.42 us  [swapped(): return lax.ppermute(x, axis, [(0, 1), (1, 0)])]
where the time goes in v5:
time: 37.6 us; the launch traced here: 37.5 us
  blocking collectives  22.2 us (59%)
  starting transfers between devices  6.42 us (17%)
  Pallas kernels  4.24 us (11%)
  waiting for transfers between devices  2.68 us (7%)
  other arithmetic  1.24 us (3%)
  between operations  0.66 us (2%)
    all_to_all x2, blocking collectives, shared(): lax.all_to_all(copies, axis, 0, 0, axis_index_groups=[MEMBERS[axis]], til...  22.2 us
    ppermute x2, starting transfers between devices, swapped(): return lax.ppermute(x, axis, [(0, 1), (1, 0)])  6.42 us
    ppermute x2, waiting for transfers between devices, swapped(): return lax.ppermute(x, axis, [(0, 1), (1, 0)])  2.68 us
    pallas_call x1, Pallas kernels, shards(): pl.pallas_call(stats_kernel, in_specs=[pl.BlockSpec(memory_space=pltpu.HB...  2.65 us
    pallas_call x1, Pallas kernels, shards(): pl.pallas_call(accumulate_kernel, in_specs=[whole] * 4, out_specs=[whole,...  0.78 us
    pallas_call x1, Pallas kernels, shards(): pl.pallas_call(lambda *refs: finish_kernel(denominator, *refs), in_specs=...  0.77 us
  transfers between devices with their start and end apart: 2, of which 2 were waited for; matrix products, arithmetic and copies ran while one was open for 3% of the time, Pallas kernels for 0%

profile of v5, /device:TPU:1, one launch (start us, length us, event | category | flops | bytes accessed | tf_op | source)
XLA Modules:
  0.0 37.5 jit_solution(15838090788015052674)
XLA Ops:
  0.6 2.6 %shard_map.58 = (f32[8,32,128]{2,1,0:T(8,128)S(1)}, bf16[4096,128]{1,0:T(8,128)(2,1)S(1)}, bf16[256,128]{1,0:T(8,128)(2,1)S(1)}, f32[32,256,128]{2,1,0:T(8,128)S(1)}, f32[32,128]{1,0:T(8,128)S(1)}) custom-call(bf16[4096,128]{1,0:T(8,128)(2,1)} %samples_hbm.1, bf16[256,128]{1,0:T(8,128)(2,1)} %centres_hbm.1, f32[2,128]{1,0:T(2,128)} %bitcast.4), custom_call_target="tpu_custom_call" | custom-call | tf_op jit(solution)/shard_map/pallas_call | solution.py:164
  3.3 9.5 %all_to_all.10.parts_ref = f32[8,32,128]{2,1,0:T(8,128)S(1)} all-to-all(f32[8,32,128]{2,1,0:T(8,128)S(1)} %get-tuple-element.15), channel_id=1, replica_groups={{5,7,6,1,4,3,2,0},{13,15,14,9,12,11,10,8},{21,23,22,17,20,19,18,16},{29..., dimensions={0} | all-to-all | bytes 262144 | tf_op jit(solution)/shard_map/all_to_all | solution.py:137
  12.8 12.8 %all_to_all.11.parts_ref = f32[8,32,128]{2,1,0:T(8,128)S(1)} all-to-all(f32[8,32,128]{2,1,0:T(8,128)S(1)} %shard_map.59), channel_id=1, replica_groups={{32,24,16,8,40,48,56,0},{33,25,17,9,41,49,57,1},{34,26,18,10,42,50,58,2..., dimensions={0} | all-to-all | bytes 262144 | tf_op jit(solution)/shard_map/all_to_all | solution.py:137
  25.6 0.8 %shard_map.60 = (f32[264,128]{1,0:T(8,128)S(1)}, f32[32,128]{1,0:T(8,128)S(1)}) custom-call(bf16[4096,128]{1,0:T(8,128)(2,1)S(1)} %get-tuple-element.12.samples_ref, f32[32,256,128]{2,1,0:T(8,128)S(1)} %get-tuple-element.13.scaled_ref, f32[32,128]{1,0:T(8,128)S(1)} %get-tuple-element.14.top_ref, f32[8,32,128]{2,1,0:T(8,128)S(1)} %all_to_all.11.parts_ref), custom_call_target="tpu_custom_call" | custom-call | tf_op jit(solution)/shard_map/pallas_call | solution.py:189
  26.4 2.5 %collective-permute-start = (f32[264,128]{1,0:T(8,128)S(1)}, f32[264,128]{1,0:T(8,128)S(1)}, u32[]{:S(2)}, u32[]{:S(2)}) collective-permute-start(f32[264,128]{1,0:T(8,128)S(1)} %get-tuple-element.16), channel_id=1, source_target_pairs={{0,128},{128,0},{1,129},{129,1},{2,130},{130,2},{3,131},{131,3},{4... | collective-permute-start | bytes 405512 | tf_op jit(solution)/shard_map/ppermute | solution.py:154
  28.9 0.6 %multiply_reduce_fusion = f32[4096]{0:T(1024)S(1)} fusion(bf16[4096,128]{1,0:T(8,128)(2,1)S(1)} %get-tuple-element.12.samples_ref), kind=kLoop, calls=%fused_computation | loop fusion | flops 1568768 | bytes 1064960 | tf_op jit(solution)/shard_map/reduce_sum | solution.py:202
  29.5 2.3 %collective-permute-done = f32[264,128]{1,0:T(8,128)S(1)} collective-permute-done((f32[264,128]{1,0:T(8,128)S(1)}, f32[264,128]{1,0:T(8,128)S(1)}, u32[]{:S(2)}, u32[]{:S(2)}) %collective-permute-start) | collective-permute-done | bytes 135200 | tf_op jit(solution)/shard_map/ppermute | solution.py:154
  31.8 3.9 %collective-permute-start.1 = (f32[264,128]{1,0:T(8,128)S(1)}, f32[264,128]{1,0:T(8,128)S(1)}, u32[]{:S(2)}, u32[]{:S(2)}) collective-permute-start(f32[264,128]{1,0:T(8,128)S(1)} %add.3.refs_0_), channel_id=1, source_target_pairs={{0,64},{64,0},{1,65},{65,1},{2,66},{66,2},{3,67},{67,3},{4,68},{68... | collective-permute-start | bytes 405512 | tf_op jit(solution)/shard_map/ppermute | solution.py:154
  35.7 0.6 %bitcast_subtract_fusion = f32[4096]{0:T(1024)} fusion(f32[4096]{0:T(1024)S(1)} %multiply_reduce_fusion, f32[32,128]{1,0:T(8,128)S(1)} %get-tuple-element.20), kind=kLoop, calls=%fused_computation.1 | loop fusion | flops 12288 | bytes 49152 | tf_op jit(solution)/shard_map/sub | solution.py:203
  36.3 0.4 %collective-permute-done.1.refs_1_ = f32[264,128]{1,0:T(8,128)S(1)} collective-permute-done((f32[264,128]{1,0:T(8,128)S(1)}, f32[264,128]{1,0:T(8,128)S(1)}, u32[]{:S(2)}, u32[]{:S(2)}) %collective-permute-start.1) | collective-permute-done | bytes 135200 | tf_op jit(solution)/shard_map/ppermute | solution.py:154
  36.7 0.8 %shard_map.61 = (f32[256,128]{1,0:T(8,128)}, f32[2,128]{1,0:T(2,128)}) custom-call(f32[264,128]{1,0:T(8,128)S(1)} %add.3.refs_0_, f32[264,128]{1,0:T(8,128)S(1)} %collective-permute-done.1.refs_1_, bf16[256,128]{1,0:T(8,128)(2,1)S(1)} %get-tuple-element.17.refs_2_), custom_call_target="tpu_custom_call" | custom-call | tf_op jit(solution)/shard_map/pallas_call | solution.py:207
  (2 shorter events, 0.1 us)
Async XLA Ops:
  26.4 5.4 %collective-permute-start = (f32[264,128]{1,0:T(8,128)S(1)}, f32[264,128]{1,0:T(8,128)S(1)}, u32[]{:S(2)}, u32[]{:S(2)}) collective-permute-start(f32[264,128]{1,0:T(8,128)S(1)} %get-tuple-element.16), channel_id=1, source_target_pairs={{0,128},{128,0},{1,129},{129,1},{2,130},{130,2},{3,131},{131,3},{4... | collective-permute-start | bytes 405512 | tf_op jit(solution)/shard_map/ppermute | solution.py:154
  31.8 4.9 %collective-permute-start.1 = (f32[264,128]{1,0:T(8,128)S(1)}, f32[264,128]{1,0:T(8,128)S(1)}, u32[]{:S(2)}, u32[]{:S(2)}) collective-permute-start(f32[264,128]{1,0:T(8,128)S(1)} %add.3.refs_0_), channel_id=1, source_target_pairs={{0,64},{64,0},{1,65},{65,1},{2,66},{66,2},{3,67},{67,3},{4,68},{68... | collective-permute-start | bytes 405512 | tf_op jit(solution)/shard_map/ppermute | solution.py:154

commit v6 on v5

--- a/solution.py
+++ b/solution.py
@@ -11,7 +11,7 @@
 AXES = ("xh", "core", "z", "yx")
 DP = ("xh", "core")
 CENTRE = ("z", "yx")
-MEMBERS = {"z": [4, 3, 2, 1, 5, 6, 7, 0], "yx": [5, 7, 6, 1, 4, 3, 2, 0]}
+MEMBERS = {"z": [5, 4, 3, 2, 6, 7, 0, 1], "yx": [5, 7, 6, 1, 4, 3, 2, 0]}
 
 inverse_coolness_beta = 0.0625
 LOG2E = float(np.log2(np.e))
@@ -21,6 +21,7 @@
 LANES = 128
 TILE = 256
 CHUNKS = 4
+ACC = 4
 SMALL = pltpu.CompilerParams(vmem_limit_bytes=16 << 20)
 
 
@@ -43,7 +44,7 @@
 
 
 def stats_kernel(
-    samples_hbm, centres_hbm, prior_hbm, out_ref, samples_ref, centres_ref, scaled_ref, top_ref, prior_ref, sems
+    samples_hbm, centres_hbm, prior_hbm, out_ref, samples_ref, centres_ref, scaled_ref, top_ref, prior_ref, score_ref, sems
 ):
     pairs = [(centres_hbm, centres_ref), (prior_hbm, prior_ref)]
     step = samples_ref.shape[0] // CHUNKS
@@ -67,24 +68,37 @@
             preferred_element_type=jnp.float32,
         )
 
-    def reduce(t, score):
+    def reduce(t):
+        slot = t % 2
         for h in range(TILE // LANES):
             at = t * (TILE // LANES) + h
-            half = score[:, h * LANES : (h + 1) * LANES]
-            top = jnp.max(half, axis=0, keepdims=True)
-            scaled = jnp.exp2((half - top) * CROSS2)
-            scaled_ref[at, :, :] = scaled
-            total = jnp.sum(scaled, axis=0, keepdims=True)
-            top_ref[pl.ds(at, 1), :] = top * CROSS2
-            out_ref[0, pl.ds(at, 1), :] = top * CROSS2 + jnp.log2(total)
+            lanes = slice(h * LANES, (h + 1) * LANES)
+            tops = [score_ref[slot, 8 * r : 8 * r + 8, lanes] for r in range(ACC)]
+            for r in range(ACC, local // 8):
+                tops[r % ACC] = jnp.maximum(tops[r % ACC], score_ref[slot, 8 * r : 8 * r + 8, lanes])
+            while len(tops) > 1:
+                tops = [jnp.maximum(a, c) for a, c in zip(tops[::2], tops[1::2])]
+            top = jnp.max(tops[0], axis=0, keepdims=True)
+            totals = [None] * ACC
+            for r in range(local // 8):
+                scaled = jnp.exp2((score_ref[slot, 8 * r : 8 * r + 8, lanes] - top) * CROSS2)
+                scaled_ref[at, 8 * r : 8 * r + 8, :] = scaled
+                totals[r % ACC] = scaled if totals[r % ACC] is None else totals[r % ACC] + scaled
+            while len(totals) > 1:
+                totals = [a + c for a, c in zip(totals[::2], totals[1::2])]
+            total = jnp.sum(totals[0], axis=0, keepdims=True)
+            top_ref[at : at + 1, :] = top * CROSS2
+            out_ref[0, at : at + 1, :] = top * CROSS2 + jnp.log2(total)
 
     for copy in copies[2:]:
         copy.wait()
     tiles = samples_ref.shape[0] // TILE
-    ahead = scores(0)
+    local = centres_ref.shape[0]
+    score_ref[0, :, :] = scores(0)
     for t in range(tiles):
-        score, ahead = ahead, scores(min(t + 1, tiles - 1))
-        reduce(t, score)
+        if t + 1 < tiles:
+            score_ref[(t + 1) % 2, :, :] = scores(t + 1)
+        reduce(t)
     for k in range(1, out_ref.shape[0]):
         out_ref[k, :, :] = out_ref[0, :, :]
 
@@ -175,6 +189,7 @@
         compiler_params=SMALL,
         scratch_shapes=[
             pltpu.VMEM(prior.shape, jnp.float32),
+            pltpu.VMEM((2, local, TILE), jnp.float32),
             pltpu.SemaphoreType.DMA((CHUNKS + 2,)),
         ],
     )(in_hbm(samples), in_hbm(centres), in_hbm(prior))

time: 37.6 us -> 37.2 us (0.989)
  blocking collectives: 22.2 us -> 21.8 us
    all_to_all x2, blocking collectives: 22.2 us -> 21.8 us  [shared(): lax.all_to_all(copies, axis, 0, 0, axis_index_groups=[MEMBERS[axis]], til...]
where the time goes in v6:
time: 37.2 us; the launch traced here: 37 us
  blocking collectives  21.8 us (59%)
  starting transfers between devices  6.7 us (18%)
  Pallas kernels  4.14 us (11%)
  waiting for transfers between devices  2.45 us (7%)
  other arithmetic  1.24 us (3%)
  between operations  0.66 us (2%)
    all_to_all x2, blocking collectives, shared(): lax.all_to_all(copies, axis, 0, 0, axis_index_groups=[MEMBERS[axis]], til...  21.8 us
    ppermute x2, starting transfers between devices, swapped(): return lax.ppermute(x, axis, [(0, 1), (1, 0)])  6.7 us
    pallas_call x1, Pallas kernels, shards(): pl.pallas_call(stats_kernel, in_specs=[pl.BlockSpec(memory_space=pltpu.HB...  2.54 us
    ppermute x2, waiting for transfers between devices, swapped(): return lax.ppermute(x, axis, [(0, 1), (1, 0)])  2.45 us
    pallas_call x1, Pallas kernels, shards(): pl.pallas_call(accumulate_kernel, in_specs=[whole] * 4, out_specs=[whole,...  0.78 us
    pallas_call x1, Pallas kernels, shards(): pl.pallas_call(lambda *refs: finish_kernel(denominator, *refs), in_specs=...  0.77 us
  transfers between devices with their start and end apart: 2, of which 2 were waited for; matrix products, arithmetic and copies ran while one was open for 3% of the time, Pallas kernels for 0%

profile of v6, /device:TPU:1, one launch (start us, length us, event | category | flops | bytes accessed | tf_op | source)
XLA Modules:
  0.0 37.0 jit_solution(7216799672871498793)
XLA Ops:
  0.6 2.5 %shard_map.58 = (f32[8,32,128]{2,1,0:T(8,128)S(1)}, bf16[4096,128]{1,0:T(8,128)(2,1)S(1)}, bf16[256,128]{1,0:T(8,128)(2,1)S(1)}, f32[32,256,128]{2,1,0:T(8,128)S(1)}, f32[32,128]{1,0:T(8,128)S(1)}) custom-call(bf16[4096,128]{1,0:T(8,128)(2,1)} %samples_hbm.1, bf16[256,128]{1,0:T(8,128)(2,1)} %centres_hbm.1, f32[2,128]{1,0:T(2,128)} %bitcast.4), custom_call_target="tpu_custom_call" | custom-call | tf_op jit(solution)/shard_map/pallas_call | solution.py:178
  3.2 9.5 %all_to_all.10.parts_ref = f32[8,32,128]{2,1,0:T(8,128)S(1)} all-to-all(f32[8,32,128]{2,1,0:T(8,128)S(1)} %get-tuple-element.15), channel_id=1, replica_groups={{5,7,6,1,4,3,2,0},{13,15,14,9,12,11,10,8},{21,23,22,17,20,19,18,16},{29..., dimensions={0} | all-to-all | bytes 262144 | tf_op jit(solution)/shard_map/all_to_all | solution.py:151
  12.7 12.3 %all_to_all.11.parts_ref = f32[8,32,128]{2,1,0:T(8,128)S(1)} all-to-all(f32[8,32,128]{2,1,0:T(8,128)S(1)} %shard_map.59), channel_id=1, replica_groups={{40,32,24,16,48,56,0,8},{41,33,25,17,49,57,1,9},{42,34,26,18,50,58,2,10..., dimensions={0} | all-to-all | bytes 262144 | tf_op jit(solution)/shard_map/all_to_all | solution.py:151
  25.0 0.8 %shard_map.60 = (f32[264,128]{1,0:T(8,128)S(1)}, f32[32,128]{1,0:T(8,128)S(1)}) custom-call(bf16[4096,128]{1,0:T(8,128)(2,1)S(1)} %get-tuple-element.12.samples_ref, f32[32,256,128]{2,1,0:T(8,128)S(1)} %get-tuple-element.13.scaled_ref, f32[32,128]{1,0:T(8,128)S(1)} %get-tuple-element.14.top_ref, f32[8,32,128]{2,1,0:T(8,128)S(1)} %all_to_all.11.parts_ref), custom_call_target="tpu_custom_call" | custom-call | tf_op jit(solution)/shard_map/pallas_call | solution.py:204
  25.8 2.7 %collective-permute-start = (f32[264,128]{1,0:T(8,128)S(1)}, f32[264,128]{1,0:T(8,128)S(1)}, u32[]{:S(2)}, u32[]{:S(2)}) collective-permute-start(f32[264,128]{1,0:T(8,128)S(1)} %get-tuple-element.16), channel_id=1, source_target_pairs={{0,128},{128,0},{1,129},{129,1},{2,130},{130,2},{3,131},{131,3},{4... | collective-permute-start | bytes 405512 | tf_op jit(solution)/shard_map/ppermute | solution.py:168
  28.6 0.6 %multiply_reduce_fusion = f32[4096]{0:T(1024)S(1)} fusion(bf16[4096,128]{1,0:T(8,128)(2,1)S(1)} %get-tuple-element.12.samples_ref), kind=kLoop, calls=%fused_computation | loop fusion | flops 1568768 | bytes 1064960 | tf_op jit(solution)/shard_map/reduce_sum | solution.py:217
  29.2 2.1 %collective-permute-done = f32[264,128]{1,0:T(8,128)S(1)} collective-permute-done((f32[264,128]{1,0:T(8,128)S(1)}, f32[264,128]{1,0:T(8,128)S(1)}, u32[]{:S(2)}, u32[]{:S(2)}) %collective-permute-start) | collective-permute-done | bytes 135200 | tf_op jit(solution)/shard_map/ppermute | solution.py:168
  31.3 4.0 %collective-permute-start.1 = (f32[264,128]{1,0:T(8,128)S(1)}, f32[264,128]{1,0:T(8,128)S(1)}, u32[]{:S(2)}, u32[]{:S(2)}) collective-permute-start(f32[264,128]{1,0:T(8,128)S(1)} %add.3.refs_0_), channel_id=1, source_target_pairs={{0,64},{64,0},{1,65},{65,1},{2,66},{66,2},{3,67},{67,3},{4,68},{68... | collective-permute-start | bytes 405512 | tf_op jit(solution)/shard_map/ppermute | solution.py:168
  35.2 0.6 %bitcast_subtract_fusion = f32[4096]{0:T(1024)} fusion(f32[4096]{0:T(1024)S(1)} %multiply_reduce_fusion, f32[32,128]{1,0:T(8,128)S(1)} %get-tuple-element.20), kind=kLoop, calls=%fused_computation.1 | loop fusion | flops 12288 | bytes 49152 | tf_op jit(solution)/shard_map/sub | solution.py:218
  35.8 0.4 %collective-permute-done.1.refs_1_ = f32[264,128]{1,0:T(8,128)S(1)} collective-permute-done((f32[264,128]{1,0:T(8,128)S(1)}, f32[264,128]{1,0:T(8,128)S(1)}, u32[]{:S(2)}, u32[]{:S(2)}) %collective-permute-start.1) | collective-permute-done | bytes 135200 | tf_op jit(solution)/shard_map/ppermute | solution.py:168
  36.2 0.8 %shard_map.61 = (f32[256,128]{1,0:T(8,128)}, f32[2,128]{1,0:T(2,128)}) custom-call(f32[264,128]{1,0:T(8,128)S(1)} %add.3.refs_0_, f32[264,128]{1,0:T(8,128)S(1)} %collective-permute-done.1.refs_1_, bf16[256,128]{1,0:T(8,128)(2,1)S(1)} %get-tuple-element.17.refs_2_), custom_call_target="tpu_custom_call" | custom-call | tf_op jit(solution)/shard_map/pallas_call | solution.py:222
  (2 shorter events, 0.1 us)
Async XLA Ops:
  25.8 5.4 %collective-permute-start = (f32[264,128]{1,0:T(8,128)S(1)}, f32[264,128]{1,0:T(8,128)S(1)}, u32[]{:S(2)}, u32[]{:S(2)}) collective-permute-start(f32[264,128]{1,0:T(8,128)S(1)} %get-tuple-element.16), channel_id=1, source_target_pairs={{0,128},{128,0},{1,129},{129,1},{2,130},{130,2},{3,131},{131,3},{4... | collective-permute-start | bytes 405512 | tf_op jit(solution)/shard_map/ppermute | solution.py:168
  31.3 5.0 %collective-permute-start.1 = (f32[264,128]{1,0:T(8,128)S(1)}, f32[264,128]{1,0:T(8,128)S(1)}, u32[]{:S(2)}, u32[]{:S(2)}) collective-permute-start(f32[264,128]{1,0:T(8,128)S(1)} %add.3.refs_0_), channel_id=1, source_target_pairs={{0,64},{64,0},{1,65},{65,1},{2,66},{66,2},{3,67},{67,3},{4,68},{68... | collective-permute-start | bytes 405512 | tf_op jit(solution)/shard_map/ppermute | solution.py:168

commit v7 on v6

--- a/solution.py
+++ b/solution.py
@@ -11,7 +11,7 @@
 AXES = ("xh", "core", "z", "yx")
 DP = ("xh", "core")
 CENTRE = ("z", "yx")
-MEMBERS = {"z": [5, 4, 3, 2, 6, 7, 0, 1], "yx": [5, 7, 6, 1, 4, 3, 2, 0]}
+MEMBERS = {"z": [5, 4, 3, 2, 6, 7, 0, 1], "yx": [5, 1, 7, 3, 4, 0, 6, 2]}
 
 inverse_coolness_beta = 0.0625
 LOG2E = float(np.log2(np.e))
@@ -59,11 +59,11 @@
     extended = jnp.concatenate([centres_ref[...], bias_parts(centres_ref, prior_ref)], axis=1)
     ones = jnp.ones((TILE, LANES), jnp.bfloat16)
 
-    def scores(t):
-        rows = samples_ref[pl.ds(t * TILE, TILE), :]
+    def scores(at):
+        rows = samples_ref[at, :]
         return lax.dot_general(
             extended,
-            jnp.concatenate([rows, ones], axis=1),
+            jnp.concatenate([rows, ones[: rows.shape[0], :]], axis=1),
             (((1,), (1,)), ((), ())),
             preferred_element_type=jnp.float32,
         )
@@ -94,10 +94,12 @@
         copy.wait()
     tiles = samples_ref.shape[0] // TILE
     local = centres_ref.shape[0]
-    score_ref[0, :, :] = scores(0)
+    for h in range(TILE // LANES):
+        lanes = slice(h * LANES, (h + 1) * LANES)
+        score_ref[0, :, lanes] = scores(lanes)
     for t in range(tiles):
         if t + 1 < tiles:
-            score_ref[(t + 1) % 2, :, :] = scores(t + 1)
+            score_ref[(t + 1) % 2, :, :] = scores(slice((t + 1) * TILE, (t + 2) * TILE))
         reduce(t)
     for k in range(1, out_ref.shape[0]):
         out_ref[k, :, :] = out_ref[0, :, :]

time: 37.2 us -> 37.2 us (level)
  no operation moved by 1% of the time
where the time goes in v7:
time: 37.2 us; the launch traced here: 37 us
  blocking collectives  21.8 us (59%)
  starting transfers between devices  6.75 us (18%)
  Pallas kernels  4.1 us (11%)
  waiting for transfers between devices  2.42 us (7%)
  other arithmetic  1.24 us (3%)
  between operations  0.66 us (2%)
    all_to_all x2, blocking collectives, shared(): lax.all_to_all(copies, axis, 0, 0, axis_index_groups=[MEMBERS[axis]], til...  21.8 us
    ppermute x2, starting transfers between devices, swapped(): return lax.ppermute(x, axis, [(0, 1), (1, 0)])  6.75 us
    pallas_call x1, Pallas kernels, shards(): pl.pallas_call(stats_kernel, in_specs=[pl.BlockSpec(memory_space=pltpu.HB...  2.51 us
    ppermute x2, waiting for transfers between devices, swapped(): return lax.ppermute(x, axis, [(0, 1), (1, 0)])  2.42 us
    pallas_call x1, Pallas kernels, shards(): pl.pallas_call(accumulate_kernel, in_specs=[whole] * 4, out_specs=[whole,...  0.77 us
    pallas_call x1, Pallas kernels, shards(): pl.pallas_call(lambda *refs: finish_kernel(denominator, *refs), in_specs=...  0.77 us
  transfers between devices with their start and end apart: 2, of which 2 were waited for; matrix products, arithmetic and copies ran while one was open for 3% of the time, Pallas kernels for 0%

profile of v7, /device:TPU:1, one launch (start us, length us, event | category | flops | bytes accessed | tf_op | source)
XLA Modules:
  0.0 37.0 jit_solution(1235998418240722980)
XLA Ops:
  0.6 2.5 %shard_map.58 = (f32[8,32,128]{2,1,0:T(8,128)S(1)}, bf16[4096,128]{1,0:T(8,128)(2,1)S(1)}, bf16[256,128]{1,0:T(8,128)(2,1)S(1)}, f32[32,256,128]{2,1,0:T(8,128)S(1)}, f32[32,128]{1,0:T(8,128)S(1)}) custom-call(bf16[4096,128]{1,0:T(8,128)(2,1)} %samples_hbm.1, bf16[256,128]{1,0:T(8,128)(2,1)} %centres_hbm.1, f32[2,128]{1,0:T(2,128)} %bitcast.4), custom_call_target="tpu_custom_call" | custom-call | tf_op jit(solution)/shard_map/pallas_call | solution.py:180
  3.2 9.5 %all_to_all.10.parts_ref = f32[8,32,128]{2,1,0:T(8,128)S(1)} all-to-all(f32[8,32,128]{2,1,0:T(8,128)S(1)} %get-tuple-element.15), channel_id=1, replica_groups={{5,1,7,3,4,0,6,2},{13,9,15,11,12,8,14,10},{21,17,23,19,20,16,22,18},{29..., dimensions={0} | all-to-all | bytes 262144 | tf_op jit(solution)/shard_map/all_to_all | solution.py:153
  12.7 12.4 %all_to_all.11.parts_ref = f32[8,32,128]{2,1,0:T(8,128)S(1)} all-to-all(f32[8,32,128]{2,1,0:T(8,128)S(1)} %shard_map.59), channel_id=1, replica_groups={{40,32,24,16,48,56,0,8},{41,33,25,17,49,57,1,9},{42,34,26,18,50,58,2,10..., dimensions={0} | all-to-all | bytes 262144 | tf_op jit(solution)/shard_map/all_to_all | solution.py:153
  25.0 0.8 %shard_map.60 = (f32[264,128]{1,0:T(8,128)S(1)}, f32[32,128]{1,0:T(8,128)S(1)}) custom-call(bf16[4096,128]{1,0:T(8,128)(2,1)S(1)} %get-tuple-element.12.samples_ref, f32[32,256,128]{2,1,0:T(8,128)S(1)} %get-tuple-element.13.scaled_ref, f32[32,128]{1,0:T(8,128)S(1)} %get-tuple-element.14.top_ref, f32[8,32,128]{2,1,0:T(8,128)S(1)} %all_to_all.11.parts_ref), custom_call_target="tpu_custom_call" | custom-call | tf_op jit(solution)/shard_map/pallas_call | solution.py:206
  25.8 2.8 %collective-permute-start = (f32[264,128]{1,0:T(8,128)S(1)}, f32[264,128]{1,0:T(8,128)S(1)}, u32[]{:S(2)}, u32[]{:S(2)}) collective-permute-start(f32[264,128]{1,0:T(8,128)S(1)} %get-tuple-element.16), channel_id=1, source_target_pairs={{0,128},{128,0},{1,129},{129,1},{2,130},{130,2},{3,131},{131,3},{4... | collective-permute-start | bytes 405512 | tf_op jit(solution)/shard_map/ppermute | solution.py:170
  28.6 0.6 %multiply_reduce_fusion = f32[4096]{0:T(1024)S(1)} fusion(bf16[4096,128]{1,0:T(8,128)(2,1)S(1)} %get-tuple-element.12.samples_ref), kind=kLoop, calls=%fused_computation | loop fusion | flops 1568768 | bytes 1064960 | tf_op jit(solution)/shard_map/reduce_sum | solution.py:219
  29.2 2.0 %collective-permute-done = f32[264,128]{1,0:T(8,128)S(1)} collective-permute-done((f32[264,128]{1,0:T(8,128)S(1)}, f32[264,128]{1,0:T(8,128)S(1)}, u32[]{:S(2)}, u32[]{:S(2)}) %collective-permute-start) | collective-permute-done | bytes 135200 | tf_op jit(solution)/shard_map/ppermute | solution.py:170
  31.2 4.0 %collective-permute-start.1 = (f32[264,128]{1,0:T(8,128)S(1)}, f32[264,128]{1,0:T(8,128)S(1)}, u32[]{:S(2)}, u32[]{:S(2)}) collective-permute-start(f32[264,128]{1,0:T(8,128)S(1)} %add.3.refs_0_), channel_id=1, source_target_pairs={{0,64},{64,0},{1,65},{65,1},{2,66},{66,2},{3,67},{67,3},{4,68},{68... | collective-permute-start | bytes 405512 | tf_op jit(solution)/shard_map/ppermute | solution.py:170
  35.2 0.6 %bitcast_subtract_fusion = f32[4096]{0:T(1024)} fusion(f32[4096]{0:T(1024)S(1)} %multiply_reduce_fusion, f32[32,128]{1,0:T(8,128)S(1)} %get-tuple-element.20), kind=kLoop, calls=%fused_computation.1 | loop fusion | flops 12288 | bytes 49152 | tf_op jit(solution)/shard_map/sub | solution.py:220
  35.8 0.4 %collective-permute-done.1.refs_1_ = f32[264,128]{1,0:T(8,128)S(1)} collective-permute-done((f32[264,128]{1,0:T(8,128)S(1)}, f32[264,128]{1,0:T(8,128)S(1)}, u32[]{:S(2)}, u32[]{:S(2)}) %collective-permute-start.1) | collective-permute-done | bytes 135200 | tf_op jit(solution)/shard_map/ppermute | solution.py:170
  36.2 0.8 %shard_map.61 = (f32[256,128]{1,0:T(8,128)}, f32[2,128]{1,0:T(2,128)}) custom-call(f32[264,128]{1,0:T(8,128)S(1)} %add.3.refs_0_, f32[264,128]{1,0:T(8,128)S(1)} %collective-permute-done.1.refs_1_, bf16[256,128]{1,0:T(8,128)(2,1)S(1)} %get-tuple-element.17.refs_2_), custom_call_target="tpu_custom_call" | custom-call | tf_op jit(solution)/shard_map/pallas_call | solution.py:224
  (2 shorter events, 0.1 us)
Async XLA Ops:
  25.8 5.4 %collective-permute-start = (f32[264,128]{1,0:T(8,128)S(1)}, f32[264,128]{1,0:T(8,128)S(1)}, u32[]{:S(2)}, u32[]{:S(2)}) collective-permute-start(f32[264,128]{1,0:T(8,128)S(1)} %get-tuple-element.16), channel_id=1, source_target_pairs={{0,128},{128,0},{1,129},{129,1},{2,130},{130,2},{3,131},{131,3},{4... | collective-permute-start | bytes 405512 | tf_op jit(solution)/shard_map/ppermute | solution.py:170
  31.2 5.0 %collective-permute-start.1 = (f32[264,128]{1,0:T(8,128)S(1)}, f32[264,128]{1,0:T(8,128)S(1)}, u32[]{:S(2)}, u32[]{:S(2)}) collective-permute-start(f32[264,128]{1,0:T(8,128)S(1)} %add.3.refs_0_), channel_id=1, source_target_pairs={{0,64},{64,0},{1,65},{65,1},{2,66},{66,2},{3,67},{67,3},{4,68},{68... | collective-permute-start | bytes 405512 | tf_op jit(solution)/shard_map/ppermute | solution.py:170

commit v8 on v7

--- a/solution.py
+++ b/solution.py
@@ -8,10 +8,15 @@
 from jax.sharding import PartitionSpec as P
 
 
-AXES = ("xh", "core", "z", "yx")
+AXES = ("xh", "core", "c")
 DP = ("xh", "core")
-CENTRE = ("z", "yx")
-MEMBERS = {"z": [5, 4, 3, 2, 6, 7, 0, 1], "yx": [5, 1, 7, 3, 4, 0, 6, 2]}
+CENTRE = ("c",)
+PAIRS = ((4, 5), (3, 2), (7, 6), (1, 0))
+ROWS = (2, 3, 1, 0)
+MEMBERS = {
+    "near": [[8 * z + 2 * y + x for y in ROWS for z in pair] for pair in PAIRS for x in range(2)],
+    "far": [[8 * pair[r] + 2 * y + x for pair in PAIRS for x in (1, 0)] for y in range(4) for r in range(2)],
+}
 
 inverse_coolness_beta = 0.0625
 LOG2E = float(np.log2(np.e))
@@ -150,7 +155,7 @@
 
 
 def shared(copies, axis):
-    return lax.all_to_all(copies, axis, 0, 0, axis_index_groups=[MEMBERS[axis]], tiled=True)
+    return lax.all_to_all(copies, "c", 0, 0, axis_index_groups=MEMBERS[axis], tiled=True)
 
 
 def on_chip(x):
@@ -175,14 +180,14 @@
     local = centres.shape[0]
     prior = facility_prior_logprob.reshape(local // LANES, LANES)
     lines = rows // LANES
-    near, far = "yx", "z"
+    near, far = "near", "far"
     whole = pl.BlockSpec(memory_space=pltpu.VMEM)
     copies, samples_here, centres_here, scaled, top = pl.pallas_call(
         stats_kernel,
         in_specs=[pl.BlockSpec(memory_space=pltpu.HBM)] * 3,
         out_specs=[whole] * 5,
         out_shape=(
-            pltpu.VMEM((lax.axis_size(near), lines, LANES), jnp.float32),
+            pltpu.VMEM((len(MEMBERS[near][0]), lines, LANES), jnp.float32),
             pltpu.VMEM((rows, features), samples.dtype),
             pltpu.VMEM((local, features), centres.dtype),
             pltpu.VMEM((lines, local, LANES), jnp.float32),
@@ -199,7 +204,7 @@
         merge_kernel,
         in_specs=[whole],
         out_specs=whole,
-        out_shape=pltpu.VMEM((lax.axis_size(far), lines, LANES), jnp.float32),
+        out_shape=pltpu.VMEM((len(MEMBERS[far][0]), lines, LANES), jnp.float32),
         compiler_params=SMALL,
     )(on_chip(shared(copies, near)))
     parts = shared(copies, far)
@@ -233,7 +238,7 @@
 
 
 def solution(mesh):
-    torus = Mesh(mesh.devices.reshape(2, 2, 8, 8), AXES)
+    torus = Mesh(mesh.devices.reshape(2, 2, 64), AXES)
     in_specs = (P(DP, None), P(CENTRE, None), P(CENTRE))
     out_specs = (P(CENTRE, None), P(CENTRE), P(DP))
     return jax.shard_map(

time: 37.2 us -> 37.2 us (level)
  starting transfers between devices: 6.75 us -> 6.17 us
    ppermute x2, starting transfers between devices: 6.75 us -> 6.17 us  [swapped(): return lax.ppermute(x, axis, [(0, 1), (1, 0)])]
where the time goes in v8:
time: 37.2 us; the launch traced here: 37 us
  blocking collectives  22 us (59%)
  starting transfers between devices  6.17 us (17%)
  Pallas kernels  4.11 us (11%)
  waiting for transfers between devices  2.77 us (7%)
  other arithmetic  1.24 us (3%)
  between operations  0.66 us (2%)
    all_to_all x2, blocking collectives, shared(): lax.all_to_all(copies, 'c', 0, 0, axis_index_groups=MEMBERS[axis], tiled=...  22 us
    ppermute x2, starting transfers between devices, swapped(): return lax.ppermute(x, axis, [(0, 1), (1, 0)])  6.17 us
    ppermute x2, waiting for transfers between devices, swapped(): return lax.ppermute(x, axis, [(0, 1), (1, 0)])  2.77 us
    pallas_call x1, Pallas kernels, shards(): pl.pallas_call(stats_kernel, in_specs=[pl.BlockSpec(memory_space=pltpu.HB...  2.51 us
    pallas_call x1, Pallas kernels, shards(): pl.pallas_call(accumulate_kernel, in_specs=[whole] * 4, out_specs=[whole,...  0.78 us
    pallas_call x1, Pallas kernels, shards(): pl.pallas_call(lambda *refs: finish_kernel(denominator, *refs), in_specs=...  0.77 us
  transfers between devices with their start and end apart: 2, of which 2 were waited for; matrix products, arithmetic and copies ran while one was open for 3% of the time, Pallas kernels for 0%

profile of v8, /device:TPU:1, one launch (start us, length us, event | category | flops | bytes accessed | tf_op | source)
XLA Modules:
  0.0 37.0 jit_solution(11669340576699951303)
XLA Ops:
  0.6 2.5 %shard_map.58 = (f32[8,32,128]{2,1,0:T(8,128)S(1)}, bf16[4096,128]{1,0:T(8,128)(2,1)S(1)}, bf16[256,128]{1,0:T(8,128)(2,1)S(1)}, f32[32,256,128]{2,1,0:T(8,128)S(1)}, f32[32,128]{1,0:T(8,128)S(1)}) custom-call(bf16[4096,128]{1,0:T(8,128)(2,1)} %samples_hbm.1, bf16[256,128]{1,0:T(8,128)(2,1)} %centres_hbm.1, f32[2,128]{1,0:T(2,128)} %bitcast.4), custom_call_target="tpu_custom_call" | custom-call | tf_op jit(solution)/shard_map/pallas_call | solution.py:185
  3.2 9.9 %all_to_all.10.parts_ref = f32[8,32,128]{2,1,0:T(8,128)S(1)} all-to-all(f32[8,32,128]{2,1,0:T(8,128)S(1)} %get-tuple-element.15), channel_id=1, replica_groups={{36,44,38,46,34,42,32,40},{37,45,39,47,35,43,33,41},{28,20,30,22,26,18,..., dimensions={0} | all-to-all | bytes 262144 | tf_op jit(solution)/shard_map/all_to_all | solution.py:158
  13.1 12.1 %all_to_all.11.parts_ref = f32[8,32,128]{2,1,0:T(8,128)S(1)} all-to-all(f32[8,32,128]{2,1,0:T(8,128)S(1)} %shard_map.59), channel_id=1, replica_groups={{33,32,25,24,57,56,9,8},{41,40,17,16,49,48,1,0},{35,34,27,26,59,58,11,1..., dimensions={0} | all-to-all | bytes 262144 | tf_op jit(solution)/shard_map/all_to_all | solution.py:158
  25.2 0.8 %shard_map.60 = (f32[264,128]{1,0:T(8,128)S(1)}, f32[32,128]{1,0:T(8,128)S(1)}) custom-call(bf16[4096,128]{1,0:T(8,128)(2,1)S(1)} %get-tuple-element.12.samples_ref, f32[32,256,128]{2,1,0:T(8,128)S(1)} %get-tuple-element.13.scaled_ref, f32[32,128]{1,0:T(8,128)S(1)} %get-tuple-element.14.top_ref, f32[8,32,128]{2,1,0:T(8,128)S(1)} %all_to_all.11.parts_ref), custom_call_target="tpu_custom_call" | custom-call | tf_op jit(solution)/shard_map/pallas_call | solution.py:211
  26.0 2.4 %collective-permute-start = (f32[264,128]{1,0:T(8,128)S(1)}, f32[264,128]{1,0:T(8,128)S(1)}, u32[]{:S(2)}, u32[]{:S(2)}) collective-permute-start(f32[264,128]{1,0:T(8,128)S(1)} %get-tuple-element.16), channel_id=1, source_target_pairs={{0,128},{128,0},{1,129},{129,1},{2,130},{130,2},{3,131},{131,3},{4... | collective-permute-start | bytes 405512 | tf_op jit(solution)/shard_map/ppermute | solution.py:175
  28.4 0.6 %multiply_reduce_fusion = f32[4096]{0:T(1024)S(1)} fusion(bf16[4096,128]{1,0:T(8,128)(2,1)S(1)} %get-tuple-element.12.samples_ref), kind=kLoop, calls=%fused_computation | loop fusion | flops 1568768 | bytes 1064960 | tf_op jit(solution)/shard_map/reduce_sum | solution.py:224
  29.0 2.4 %collective-permute-done = f32[264,128]{1,0:T(8,128)S(1)} collective-permute-done((f32[264,128]{1,0:T(8,128)S(1)}, f32[264,128]{1,0:T(8,128)S(1)}, u32[]{:S(2)}, u32[]{:S(2)}) %collective-permute-start) | collective-permute-done | bytes 135200 | tf_op jit(solution)/shard_map/ppermute | solution.py:175
  31.5 3.8 %collective-permute-start.1 = (f32[264,128]{1,0:T(8,128)S(1)}, f32[264,128]{1,0:T(8,128)S(1)}, u32[]{:S(2)}, u32[]{:S(2)}) collective-permute-start(f32[264,128]{1,0:T(8,128)S(1)} %add.3.refs_0_), channel_id=1, source_target_pairs={{0,64},{64,0},{1,65},{65,1},{2,66},{66,2},{3,67},{67,3},{4,68},{68... | collective-permute-start | bytes 405512 | tf_op jit(solution)/shard_map/ppermute | solution.py:175
  35.2 0.6 %bitcast_subtract_fusion = f32[4096]{0:T(1024)} fusion(f32[4096]{0:T(1024)S(1)} %multiply_reduce_fusion, f32[32,128]{1,0:T(8,128)S(1)} %get-tuple-element.20), kind=kLoop, calls=%fused_computation.1 | loop fusion | flops 12288 | bytes 49152 | tf_op jit(solution)/shard_map/sub | solution.py:225
  35.8 0.4 %collective-permute-done.1.refs_1_ = f32[264,128]{1,0:T(8,128)S(1)} collective-permute-done((f32[264,128]{1,0:T(8,128)S(1)}, f32[264,128]{1,0:T(8,128)S(1)}, u32[]{:S(2)}, u32[]{:S(2)}) %collective-permute-start.1) | collective-permute-done | bytes 135200 | tf_op jit(solution)/shard_map/ppermute | solution.py:175
  36.2 0.8 %shard_map.61 = (f32[256,128]{1,0:T(8,128)}, f32[2,128]{1,0:T(2,128)}) custom-call(f32[264,128]{1,0:T(8,128)S(1)} %add.3.refs_0_, f32[264,128]{1,0:T(8,128)S(1)} %collective-permute-done.1.refs_1_, bf16[256,128]{1,0:T(8,128)(2,1)S(1)} %get-tuple-element.17.refs_2_), custom_call_target="tpu_custom_call" | custom-call | tf_op jit(solution)/shard_map/pallas_call | solution.py:229
  (2 shorter events, 0.1 us)
Async XLA Ops:
  26.0 5.4 %collective-permute-start = (f32[264,128]{1,0:T(8,128)S(1)}, f32[264,128]{1,0:T(8,128)S(1)}, u32[]{:S(2)}, u32[]{:S(2)}) collective-permute-start(f32[264,128]{1,0:T(8,128)S(1)} %get-tuple-element.16), channel_id=1, source_target_pairs={{0,128},{128,0},{1,129},{129,1},{2,130},{130,2},{3,131},{131,3},{4... | collective-permute-start | bytes 405512 | tf_op jit(solution)/shard_map/ppermute | solution.py:175
  31.5 4.7 %collective-permute-start.1 = (f32[264,128]{1,0:T(8,128)S(1)}, f32[264,128]{1,0:T(8,128)S(1)}, u32[]{:S(2)}, u32[]{:S(2)}) collective-permute-start(f32[264,128]{1,0:T(8,128)S(1)} %add.3.refs_0_), channel_id=1, source_target_pairs={{0,64},{64,0},{1,65},{65,1},{2,66},{66,2},{3,67},{67,3},{4,68},{68... | collective-permute-start | bytes 405512 | tf_op jit(solution)/shard_map/ppermute | solution.py:175
